TPU v7x, 256 devices: a whole 4x4x8 slice. The times are simulated.
256 devices in a mesh: gz: 64 (over z, x, core), gy: 4 (over y).
Axes of the slice: x: 4, y: 4, z: 8, core: 2. Of those that a mesh axis runs over, the one named last changes fastest.
Arguments:
- iterate: float32 [128, 256, 1024], P('gz', 'gy'), may hold values from -1.5 to 1.5
- basis: bfloat16 [32, 128, 256, 1024], P(None, 'gz', 'gy'), may hold values from -6 to 6
- coeffs: float32 [32], replicated, may hold values from -0.3125 to 0.3125
- rhs: float32 [128, 256, 1024], P('gz', 'gy'), may hold values from -8 to 8
- kappa: float32 [128, 256, 1024], P('gz', 'gy'), may hold values from 0.5 to 4
- offsets: int32 [128, 256, 8], P('gz', 'gy'), may hold values from 0 to 2047
- flips: int32 [128, 256, 8], P('gz', 'gy'), may hold values from 0 to 1
Outputs:
- new_iterate: float32 [128, 256, 1024], P('gz', 'gy')
- residual: float32 [128, 256, 1024], P('gz', 'gy')
- sketch_unit: float32 [2048], replicated
All inputs are finite; a program needn't handle non-finite values.
Results may differ from a plain program's by a relative error of at most 0.00058.
Values sent between devices are 32-bit elements; how exact they have to be, the bound alone decides.
No kernel may reach another device: no remote copies, remote signals or barrier semaphores. Data moves between devices by JAX's collectives and lax.ppermute only.
A program may use at most 64 MiB of HBM per device.

v0:
```python
import functools

import jax
import jax.numpy as jnp
from jax import lax
from jax.experimental import pallas as pl
from jax.experimental.pallas import tpu as pltpu
from jax.sharding import Mesh
from jax.sharding import PartitionSpec as P


SK = 2048
BLK = 128
ROWS = SK // BLK
GROUP = 4
GZ = ("z", "x", "core")
HBM = pl.BlockSpec(memory_space=pltpu.HBM)
VMEM = pl.BlockSpec(memory_space=pltpu.VMEM)


def f32(*shape):
    return jax.ShapeDtypeStruct(shape, jnp.float32)


def parities():
    return lax.axis_index("core") == 0, lax.rem(lax.axis_index("gy"), 2) == 0


def columns(table):
    return jnp.transpose(table)


def spread(column, q, height):
    return jnp.broadcast_to(column[:, q : q + 1], (height, BLK))


def edge_kernel(k_hbm, off_hbm, flip_hbm, same_ref, cross_ref, even_ref, odd_ref, k_ref, off_ref, flip_ref, sems):
    copies = [
        pltpu.make_async_copy(source, target, sems.at[i])
        for i, (source, target) in enumerate(((k_hbm, k_ref), (off_hbm, off_ref), (flip_hbm, flip_ref)))
    ]
    for copy in copies:
        copy.start()
    for copy in copies:
        copy.wait()
    nz, ny, nx = k_ref.shape
    blocks = nx // BLK
    core0, even = parities()

    def both(low, high):
        return jnp.where(core0, high, low), jnp.where(core0, low, high)

    same_ref[:ny], cross_ref[:ny] = both(k_ref[0], k_ref[1])
    offs = [off_ref[z].astype(jnp.float32) for z in range(nz)]
    signs = [(2 * flip_ref[z] - 1).astype(jnp.float32) for z in range(nz)]
    same_ref[ny:, :ny], cross_ref[ny:, :ny] = both(offs[0], offs[1])
    same_ref[ny:, BLK : BLK + ny], cross_ref[ny:, BLK : BLK + ny] = both(signs[0], signs[1])
    for z in range(nz):
        off_t, sign_t = columns(offs[z]), columns(signs[z])
        for q in range(blocks):
            lanes = slice(q * BLK, (q + 1) * BLK)
            for at, table in ((nz + z, off_t), (2 * nz + z, sign_t)):
                low = jnp.broadcast_to(table[:1, q : q + 1], (1, BLK))
                high = jnp.broadcast_to(table[ny - 1 :, q : q + 1], (1, BLK))
                even_ref[at : at + 1, lanes] = jnp.where(even, high, low)
                odd_ref[at : at + 1, lanes] = jnp.where(even, low, high)
        low, high = k_ref[z, :1, :], k_ref[z, ny - 1 :, :]
        even_ref[z : z + 1, :] = jnp.where(even, high, low)
        odd_ref[z : z + 1, :] = jnp.where(even, low, high)
    rest = slice(3 * nz, 8)
    even_ref[rest, :] = jnp.zeros((8 - 3 * nz, nx), jnp.float32)
    odd_ref[rest, :] = jnp.zeros((8 - 3 * nz, nx), jnp.float32)


def edges(kappa, offsets, flips):
    _, ny, nx = kappa.shape
    plane, line = f32(ny + 8, nx), f32(8, nx)
    return pl.pallas_call(
        edge_kernel,
        out_shape=(plane, plane, line, line),
        in_specs=[HBM] * 3,
        out_specs=(VMEM,) * 4,
        scratch_shapes=[pltpu.VMEM(v.shape, v.dtype) for v in (kappa, offsets, flips)] + [pltpu.SemaphoreType.DMA((3,))],
        compiler_params=pltpu.CompilerParams(vmem_limit_bytes=8 << 20),
        cost_estimate=pl.CostEstimate(flops=1 << 32, bytes_accessed=1 << 28, transcendentals=0),
        name="edges",
    )(*(pltpu.with_memory_space_constraint(v, pltpu.HBM) for v in (kappa, offsets, flips)))


def update_kernel(coeff_ref, iterate_ref, basis_ref, u_ref, uc_ref, splat):
    kb, nz, ny, nx = basis_ref.shape
    core0, _ = parities()
    rounded = coeff_ref[...].astype(jnp.bfloat16).astype(jnp.float32)
    for k in range(kb):
        splat[k] = jnp.broadcast_to(rounded[:, k : k + 1], (8, BLK))

    @pl.loop(0, ny // 16)
    def _(i):
        rows = pl.ds(pl.multiple_of(i * 16, 16), 16)

        @pl.loop(0, nx // (2 * BLK))
        def _(j):
            lanes = [pl.ds(pl.multiple_of((2 * j + h) * BLK, BLK), BLK) for h in range(2)]
            spots = [(z, rows, part) for z in range(nz) for part in lanes]
            acc = [iterate_ref[spot] for spot in spots]
            for k in range(kb):
                scale = jnp.concatenate([splat[k]] * 2, 0)
                for n, spot in enumerate(spots):
                    acc[n] = acc[n] + scale * basis_ref[(k, *spot)].astype(jnp.float32)
            for n, spot in enumerate(spots):
                u_ref[spot] = acc[n]
            for n, part in enumerate(lanes):
                uc_ref[rows, part] = jnp.where(core0, acc[n], acc[len(lanes) + n])


def update(coeffs, iterate, basis):
    kb = basis.shape[0]
    return pl.pallas_call(
        update_kernel,
        out_shape=(f32(*iterate.shape), f32(*iterate.shape[1:])),
        in_specs=[VMEM] * 3,
        out_specs=(VMEM, VMEM),
        scratch_shapes=[pltpu.VMEM((kb, 8, BLK), jnp.float32)],
        compiler_params=pltpu.CompilerParams(vmem_limit_bytes=16 << 20),
        cost_estimate=pl.CostEstimate(flops=1 << 24, bytes_accessed=2 * basis.size, transcendentals=0),
        name="update",
    )(coeffs.reshape(1, kb), iterate, basis)


def lane_gather(values, index):
    numbers = lax.GatherDimensionNumbers(
        offset_dims=(),
        collapsed_slice_dims=(1,),
        start_index_map=(1,),
        operand_batching_dims=(0,),
        start_indices_batching_dims=(0,),
    )
    return lax.gather(values, index[..., None], numbers, (1, 1), mode=lax.GatherScatterMode.PROMISE_IN_BOUNDS)


def sketch_kernel(
    u_ref, k_ref, rhs_ref, off_ref, flip_ref, same_ref, cross_ref, even_ref, odd_ref,
    out_ref, us_ref, ue_ref, uo_ref, base_ref, wz_ref, wy_ref,
    hz_ref, hy_ref, sem,
):
    nz, ny, nx = u_ref.shape
    core0, even = parities()
    blocks = nx // BLK
    store = pltpu.make_async_copy(u_ref, out_ref, sem)
    store.start()

    for z in range(nz):
        low, high = u_ref[z, :1, :], u_ref[z, ny - 1 :, :]
        ue_ref[z : z + 1, :] = jnp.where(even, high, low)
        uo_ref[z : z + 1, :] = jnp.where(even, low, high)

    lane = lax.broadcasted_iota(jnp.int32, (8, BLK), 1)
    line = lax.broadcasted_iota(jnp.int32, (8, BLK), 0)
    low_y = jnp.where(even, odd_ref[...], even_ref[...])
    high_y = jnp.where(even, even_ref[...], odd_ref[...])
    cells = [(z, q) for z in range(nz) for q in range(blocks)]

    def lanes(q):
        return slice(q * BLK, (q + 1) * BLK)

    def tile(ref, y):
        return {(z, q): ref[z, y : y + 8, lanes(q)] for z, q in cells}

    def up(tiles):
        return {c: pltpu.roll(t, 7, 0) for c, t in tiles.items()}

    u, k = tile(u_ref, 0), tile(k_ref, 0)
    u_up, k_up = up(u), up(k)
    below = None
    for y in range(0, ny, 8):
        rows = slice(y, y + 8)
        if y + 8 < ny:
            u_next, k_next = tile(u_ref, y + 8), tile(k_ref, y + 8)
            u_next_up, k_next_up = up(u_next), up(k_next)
        else:
            u_next = k_next = None
            u_next_up = {c: 0.0 for c in cells}
            k_next_up = {(z, q): high_y[z : z + 1, lanes(q)] for z, q in cells}
        between = {q: (k[0, q] + k[1, q]) * (u[0, q] - u[1, q]) for q in range(blocks)}
        above = {}
        for z in range(nz):
            swap = core0 if z else jnp.logical_not(core0)
            u_right = {q: pltpu.roll(u[z, q], BLK - 1, 1) for q in range(blocks)}
            k_right = {q: pltpu.roll(k[z, q], BLK - 1, 1) for q in range(blocks)}
            u_right[blocks] = k_right[blocks] = 0.0
            left = None
            for q in range(blocks):
                c = (z, q)
                pair = k[c] + jnp.where(swap, same_ref[rows, lanes(q)], cross_ref[rows, lanes(q)])
                wz = 0.5 * pair
                wz_ref[z, rows, lanes(q)] = wz
                hz_ref[z, rows, lanes(q)] = wz * u[c]
                total = pair * u[c]
                total = total - between[q] if z else total + between[q]
                flow = (k[c] + jnp.where(line == 7, k_next_up[c], k_up[c])) * (
                    u[c] - jnp.where(line == 7, u_next_up[c], u_up[c])
                )
                above[c] = pltpu.roll(flow, 1, 0)
                if y == 0:
                    edge = k[c] + low_y[z : z + 1, lanes(q)]
                    wy_ref[z : z + 1, lanes(q)] = 0.5 * edge[:1]
                    edge = edge * u[c]
                    hy_ref[z : z + 1, lanes(q)] = 0.5 * edge[:1]
                    before = -edge
                else:
                    before = below[c]
                if y == ny - 8:
                    edge = k[c] + high_y[z : z + 1, lanes(q)]
                    wy_ref[nz + z : nz + z + 1, lanes(q)] = 0.5 * edge[7:]
                    hy_ref[nz + z : nz + z + 1, lanes(q)] = 0.5 * (edge * u[c])[7:]
                total = total + (flow - jnp.where(line == 0, before, above[c]))
                flow = (k[c] + jnp.where(lane == BLK - 1, k_right[q + 1], k_right[q])) * (
                    u[c] - jnp.where(lane == BLK - 1, u_right[q + 1], u_right[q])
                )
                turned = pltpu.roll(flow, 1, 1)
                before = -k[c] * u[c] if q == 0 else left
                total = total + (flow - jnp.where(lane == 0, before, turned))
                left = turned
                base_ref[z, rows, lanes(q)] = (rhs_ref[z, rows, lanes(q)] - 0.05 * u[c]) - 0.5 * total
        below = above
        u, k, u_up, k_up = u_next, k_next, u_next_up, k_next_up

    for y in range(0, ny, 8):
        rows = slice(y, y + 8)
        us_ref[rows, :] = jnp.where(core0, u_ref[1, rows, :], u_ref[0, rows, :])

    sums = []

    def place(offs, signs):
        slot = lax.broadcasted_iota(jnp.int32, (ROWS, offs.shape[1]), 0)
        return jnp.where(slot == jnp.right_shift(offs, 7), signs, 0.0).astype(jnp.bfloat16)

    def turn(block, by):
        spot = lax.broadcasted_iota(jnp.int32, block.shape, 1)
        here = spot >= by
        block = lane_gather(block, (spot - by) & (BLK - 1))
        high = block.astype(jnp.bfloat16)
        low = (block - high.astype(jnp.float32)).astype(jnp.bfloat16)
        none = jnp.zeros_like(high)
        return [jnp.concatenate([jnp.where(here, t, none), jnp.where(here, none, t)], 1) for t in (high, low)]

    def add(spots, terms):
        at = jnp.concatenate(spots * 2, 1)
        values = jnp.concatenate([t[0] for t in terms] + [t[1] for t in terms], 0)
        sums.append(jnp.dot(at, values, preferred_element_type=jnp.float32))

    for z in range(nz):
        swap = core0 if z else jnp.logical_not(core0)
        theirs = jnp.where(swap, same_ref[ny:, : 2 * BLK], cross_ref[ny:, : 2 * BLK])
        mine = (2 * flip_ref[z] - 1).astype(jnp.float32)
        for source, offs, signs in (
            (base_ref, off_ref[z], mine),
            (hz_ref, theirs[:, :ny].astype(jnp.int32), theirs[:, BLK : BLK + ny]),
        ):
            turned = columns(offs & (BLK - 1))
            for start in range(0, blocks, GROUP):
                group = range(start, start + GROUP)
                at = place(
                    jnp.concatenate([offs[q : q + 1, :] for q in group], 1),
                    jnp.concatenate([signs[q : q + 1, :] for q in group], 1),
                )
                add([at], [turn(source[z, :, lanes(q)], spread(turned, q, ny)) for q in group])

    hy_ref[2 * nz :, :] = jnp.zeros((16 - 2 * nz, nx), jnp.float32)
    unused = jnp.zeros((16 - 2 * nz, nx), jnp.float32)
    y_offs = jnp.concatenate([low_y[nz : 2 * nz], high_y[nz : 2 * nz], unused], 0).astype(jnp.int32)
    y_signs = jnp.concatenate([low_y[2 * nz : 3 * nz], high_y[2 * nz : 3 * nz], unused], 0)
    spots, terms = [], []
    for q in range(blocks):
        offs, signs = y_offs[:, lanes(q)], y_signs[:, lanes(q)]
        spots.append(place(jnp.transpose(offs[:, :1]), jnp.transpose(signs[:, :1])))
        terms.append(turn(hy_ref[:, lanes(q)], offs & (BLK - 1)))
    add(spots, terms)

    got = sum(sums[1:], sums[0])
    carry = got[:, BLK:]
    part = got[:, :BLK] + jnp.concatenate([carry[ROWS - 1 :], carry[: ROWS - 1]], 0)
    us_ref[ny:, :] = jnp.zeros((8, nx), jnp.float32)
    for m in range(ROWS):
        at = ny + m // blocks
        us_ref[at : at + 1, lanes(m % blocks)] = part[m : m + 1]
    store.wait()


def sketch(u, *rest):
    nz, ny, nx = u.shape
    field = f32(nz, ny, nx)
    return pl.pallas_call(
        sketch_kernel,
        out_shape=(field, f32(ny + 8, nx), f32(nz, nx), f32(nz, nx), field, field, f32(2 * nz, nx)),
        in_specs=[VMEM] * 9,
        out_specs=(pl.BlockSpec(memory_space=pl.ANY),) + (VMEM,) * 6,
        scratch_shapes=[
            pltpu.VMEM((nz, ny, nx), jnp.float32),
            pltpu.VMEM((16, nx), jnp.float32),
            pltpu.SemaphoreType.DMA,
        ],
        compiler_params=pltpu.CompilerParams(vmem_limit_bytes=16 << 20),
        cost_estimate=pl.CostEstimate(flops=1 << 24, bytes_accessed=16 << 20, transcendentals=0),
        name="sketch",
    )(u, *rest)


def halo_kernel(base_ref, wz_ref, wy_ref, us_ref, uc_ref, ue_ref, uo_ref, res_ref):
    nz, ny, _ = base_ref.shape
    core0, even = parities()
    low_y = jnp.where(even, uo_ref[...], ue_ref[...])
    high_y = jnp.where(even, ue_ref[...], uo_ref[...])
    for z in range(nz):
        swap = core0 if z else jnp.logical_not(core0)
        for y in range(0, ny, 8):
            rows = slice(y, y + 8)
            value = base_ref[z, rows, :] + wz_ref[z, rows, :] * jnp.where(swap, us_ref[rows, :], uc_ref[rows, :])
            res_ref[z, rows, :] = value
        res_ref[z, :1, :] += wy_ref[z : z + 1, :] * low_y[nz + z : nz + z + 1, :]
        res_ref[z, ny - 1 :, :] += wy_ref[nz + z : nz + z + 1, :] * high_y[nz + z : nz + z + 1, :]


def with_halo(base, *rest):
    return pl.pallas_call(
        halo_kernel,
        out_shape=f32(*base.shape),
        in_specs=[VMEM] * 7,
        out_specs=VMEM,
        compiler_params=pltpu.CompilerParams(vmem_limit_bytes=8 << 20),
        cost_estimate=pl.CostEstimate(flops=1 << 20, bytes_accessed=2 << 20, transcendentals=0),
        name="halo",
    )(base, *rest)


def scale_kernel(*refs):
    sketch = refs[0][...]
    for ref in refs[1:-1]:
        sketch = sketch + ref[...]
    mean = jnp.sum(sketch * sketch) * (1.0 / SK)
    unit = sketch / jnp.sqrt(jnp.broadcast_to(mean + 1e-06, sketch.shape))
    wide = sketch.shape[1] // BLK
    for m in range(ROWS):
        refs[-1][m : m + 1, :] = unit[m // wide : m // wide + 1, m % wide * BLK : (m % wide + 1) * BLK]


def scaled(*parts):
    return pl.pallas_call(
        scale_kernel,
        out_shape=f32(ROWS, BLK),
        in_specs=[VMEM] * len(parts),
        out_specs=VMEM,
        compiler_params=pltpu.CompilerParams(vmem_limit_bytes=4 << 20),
        name="scaled",
    )(*parts)


def both_ways(pairs):
    return pairs + [(b, a) for a, b in pairs]


def pairs_from(first, count):
    return both_ways([(i, i + 1) for i in range(first, count - 1, 2)])


def rounds(count):
    pairs = {"pair": pairs_from(0, count)}
    if count == 2:
        return [pairs]
    if count == 4:
        return [pairs, {"far": [(2, 0), (1, 3)], "near": pairs_from(1, count)}]
    third = both_ways([(0, 5), (1, 4), (2, 7), (3, 6)])
    second = [(i, (i - 2) % 8) for i in range(0, 8, 2)] + [(i, (i + 2) % 8) for i in range(1, 8, 2)]
    first = both_ways([(i, (i + 1) % 8) for i in range(1, 8, 2)])
    return [pairs, {"third": third, "second": second, "first": first}]


def shards(sizes, *arrays):
    return cycle_end(sizes, *arrays)


def cycle_end(sizes, iterate, basis, coeffs, rhs, kappa, offsets, flips):
    gz = sizes["z"] * sizes["x"] * sizes["core"]
    gy = sizes["gy"]
    _, ny, _ = kappa.shape
    same, cross = pairs_from(0, gz), pairs_from(1, gz)
    even, odd = pairs_from(0, gy), pairs_from(1, gy)

    offsets, flips = jnp.swapaxes(offsets, 1, 2), jnp.swapaxes(flips, 1, 2)
    k_same, k_cross, k_even, k_odd = edges(kappa, offsets, flips)
    k_cross = lax.ppermute(k_cross, GZ, cross)
    k_same = lax.ppermute(k_same, GZ, same)
    k_even = lax.ppermute(k_even, "gy", even)
    k_odd = lax.ppermute(k_odd, "gy", odd)
    u, u_cross = update(coeffs, iterate, basis)
    u_cross = lax.ppermute(u_cross, GZ, cross)
    u_out, u_same, u_even, u_odd, base, wz, wy = sketch(u, kappa, rhs, offsets, flips, k_same, k_cross, k_even, k_odd)
    got = lax.ppermute(u_same, GZ, same)
    value = u_same[ny : ny + 2] + got[ny : ny + 2]
    u_same = got
    u_even = lax.ppermute(jnp.concatenate([value, u_even], 0), "gy", even)
    value = value + u_even[:2]
    far = lax.ppermute(value, "gy", rounds(gy)[1]["far"])
    u_odd = lax.ppermute(jnp.concatenate([value, u_odd], 0), "gy", odd)
    value = value + far + u_odd[:2]
    terms = [value]
    for axis in ("x", "z"):
        for step in rounds(sizes[axis]) if sizes[axis] > 1 else ():
            value = sum(terms[1:], terms[0])
            terms = [value] + [lax.ppermute(value, axis, pairs) for pairs in step.values()]
    residual = with_halo(base, wz, wy, u_same, u_cross, u_even, u_odd)
    return u_out, residual, scaled(*terms).reshape(SK)


def build(mesh, outer):
    gy = mesh.shape["gy"]
    finer = Mesh(mesh.devices.reshape(*outer, gy), (*GZ, "gy"))
    sizes = dict(finer.shape)
    field = P(GZ, "gy", None)
    return jax.shard_map(
        functools.partial(shards, sizes),
        mesh=finer,
        in_specs=(field, P(None, GZ, "gy", None), P(), field, field, field, field),
        out_specs=(field, field, P()),
        check_vma=False,
    )


def solution(mesh):
    return build(mesh, (mesh.shape["gz"] // 8, 4, 2))
```

profile of v0, /device:TPU:8, one launch (start us, length us, event | category | flops | bytes accessed | tf_op | source)
XLA Modules:
  0.0 62.6 jit_solution(988982832729506890)
XLA Ops:
  0.6 0.0 copy-start.5
  0.6 0.0 slice-start
  0.7 0.0 copy-start
  0.7 0.0 slice-start.1
  0.7 1.5 %edges.1 = (f32[72,1024]{1,0:T(8,128)S(1)}, f32[72,1024]{1,0:T(8,128)S(1)}, f32[8,1024]{1,0:T(8,128)S(1)}, f32[8,1024]{1,0:T(8,128)S(1)}) custom-call(f32[2,64,1024]{2,1,0:T(8,128)} %k_ref.1, s32[2,8,64]{2,1,0:T(8,128)} %bitcast.6, s32[2,8,64]{2,1,0:T(8,128)} %bitcast.8), custom_call_target="tpu_custom_call" | custom-call | flops 4294967296 | bytes 268435456 | tf_op jit(solution)/shard_map/edges/pallas_call | solution.py:78
  2.2 0.0 copy-start.1
  2.2 0.0 copy-start.2
  2.2 0.0 copy-start.3
  2.2 0.0 copy-start.4
  2.2 0.1 collective-permute-start
  2.3 0.8 %collective-permute-start.1 = (f32[72,1024]{1,0:T(8,128)S(1)}, f32[72,1024]{1,0:T(8,128)S(1)}, u32[]{:S(2)}, u32[]{:S(2)}) collective-permute-start(f32[72,1024]{1,0:T(8,128)S(1)} %get-tuple-element.18), channel_id=1, source_target_pairs={{4,8},{12,16},{20,24},{28,32},{36,40},{44,48},{52,56},{60,64},{68,... | collective-permute-start | bytes 884744 | tf_op jit(solution)/shard_map/ppermute | solution.py:391
  3.2 2.2 %collective-permute-start.2 = (f32[8,1024]{1,0:T(8,128)S(1)}, f32[8,1024]{1,0:T(8,128)S(1)}, u32[]{:S(2)}, u32[]{:S(2)}) collective-permute-start(f32[8,1024]{1,0:T(8,128)S(1)} %get-tuple-element.19), channel_id=1, source_target_pairs={{0,1},{2,3},{1,0},{3,2},{4,5},{6,7},{5,4},{7,6},{8,9},{10,11},{9,8... | collective-permute-start | bytes 98312 | tf_op jit(solution)/shard_map/ppermute | solution.py:393
  5.4 2.6 %collective-permute-start.3 = (f32[8,1024]{1,0:T(8,128)S(1)}, f32[8,1024]{1,0:T(8,128)S(1)}, u32[]{:S(2)}, u32[]{:S(2)}) collective-permute-start(f32[8,1024]{1,0:T(8,128)S(1)} %get-tuple-element.20), channel_id=1, source_target_pairs={{1,2},{2,1},{5,6},{6,5},{9,10},{10,9},{13,14},{14,13},{17,18},{18,... | collective-permute-start | bytes 98312 | tf_op jit(solution)/shard_map/ppermute | solution.py:394
  8.0 0.0 copy-done.5
  8.0 0.0 slice-done
  8.0 0.0 copy-done
  8.0 0.0 slice-done.1
  8.1 2.8 %update.1 = (f32[2,64,1024]{2,1,0:T(8,128)S(1)}, f32[64,1024]{1,0:T(8,128)S(1)}) custom-call(f32[1,32]{1,0:T(1,128)S(1)} %bitcast.10, f32[2,64,1024]{2,1,0:T(8,128)S(1)} %copy-done, bf16[32,2,64,1024]{3,2,1,0:T(8,128)(2,1)S(1)} %bitcast.5), custom_call_target="tpu_custom_call" | custom-call | flops 16777216 | bytes 8388608 | tf_op jit(solution)/shard_map/update/pallas_call | solution.py:118
  10.8 0.0 collective-permute-done.2.even_ref
  10.8 0.4 collective-permute-done.3.odd_ref
  11.2 0.0 collective-permute-done.same_ref
  11.2 0.0 collective-permute-done.1.cross_ref
  11.2 0.0 copy-done.1
  11.2 0.0 copy-done.2
  11.2 0.0 copy-done.3
  11.2 0.0 copy-done.4
  11.2 4.4 %sketch.1 = (f32[2,64,1024]{2,1,0:T(8,128)}, f32[72,1024]{1,0:T(8,128)S(1)}, f32[2,1024]{1,0:T(2,128)S(1)}, f32[2,1024]{1,0:T(2,128)S(1)}, f32[2,64,1024]{2,1,0:...) custom-call(f32[2,64,1024]{2,1,0:T(8,128)S(1)} %get-tuple-element.16.u_ref, ...), custom_call_target="tpu_custom_call" | custom-call | flops 16777216 | bytes 16777216 | tf_op jit(solution)/shard_map/sketch/pallas_call | solution.py:293
  15.6 2.2 %collective-permute-start.4 = (f32[72,1024]{1,0:T(8,128)S(1)}, f32[72,1024]{1,0:T(8,128)S(1)}, u32[]{:S(2)}, u32[]{:S(2)}) collective-permute-start(f32[72,1024]{1,0:T(8,128)S(1)} %get-tuple-element.25), channel_id=1, source_target_pairs={{0,4},{8,12},{16,20},{24,28},{32,36},{40,44},{48,52},{56,60},{64,6... | collective-permute-start | bytes 884744 | tf_op jit(solution)/shard_map/ppermute | solution.py:398
  17.8 1.2 %collective-permute-done.4.us_ref = f32[72,1024]{1,0:T(8,128)S(1)} collective-permute-done((f32[72,1024]{1,0:T(8,128)S(1)}, f32[72,1024]{1,0:T(8,128)S(1)}, u32[]{:S(2)}, u32[]{:S(2)}) %collective-permute-start.4) | collective-permute-done | bytes 294944 | tf_op jit(solution)/shard_map/ppermute | solution.py:398
  19.0 0.1 collective-permute-start.6
  19.1 3.7 %collective-permute-done.6.ue_ref = f32[4,1024]{1,0:T(4,128)S(1)} collective-permute-done((f32[4,1024]{1,0:T(4,128)S(1)}, f32[4,1024]{1,0:T(4,128)S(1)}, u32[]{:S(2)}, u32[]{:S(2)}) %collective-permute-start.6) | collective-permute-done | bytes 16416 | tf_op jit(solution)/shard_map/ppermute | solution.py:401
  22.9 2.2 %collective-permute-start.7 = (f32[4,1024]{1,0:T(4,128)S(1)}, f32[4,1024]{1,0:T(4,128)S(1)}, u32[]{:S(2)}, u32[]{:S(2)}) collective-permute-start(f32[4,1024]{1,0:T(4,128)S(1)} %pad_maximum_fusion.1), channel_id=1, source_target_pairs={{1,2},{2,1},{5,6},{6,5},{9,10},{10,9},{13,14},{14,13},{17,18},{18,... | collective-permute-start | bytes 49160 | tf_op jit(solution)/shard_map/ppermute | solution.py:404
  25.1 1.3 %collective-permute-start.8 = (f32[2,1024]{1,0:T(2,128)S(1)}, f32[2,1024]{1,0:T(2,128)S(1)}, u32[]{:S(2)}, u32[]{:S(2)}) collective-permute-start(f32[2,1024]{1,0:T(2,128)S(1)} %slice_add_fusion.1), channel_id=1, source_target_pairs={{2,0},{1,3},{6,4},{5,7},{10,8},{9,11},{14,12},{13,15},{18,16},{17,... | collective-permute-start | bytes 24584 | tf_op jit(solution)/shard_map/ppermute | solution.py:403
  26.4 0.7 %collective-permute-start.5 = (f32[64,1024]{1,0:T(8,128)S(1)}, f32[64,1024]{1,0:T(8,128)S(1)}, u32[]{:S(2)}, u32[]{:S(2)}) collective-permute-start(f32[64,1024]{1,0:T(8,128)S(1)} %get-tuple-element.26), channel_id=1, source_target_pairs={{4,8},{12,16},{20,24},{28,32},{36,40},{44,48},{52,56},{60,64},{68,... | collective-permute-start | bytes 786440 | tf_op jit(solution)/shard_map/ppermute | solution.py:396
  27.1 0.7 %collective-permute-done.8 = f32[2,1024]{1,0:T(2,128)S(1)} collective-permute-done((f32[2,1024]{1,0:T(2,128)S(1)}, f32[2,1024]{1,0:T(2,128)S(1)}, u32[]{:S(2)}, u32[]{:S(2)}) %collective-permute-start.8) | collective-permute-done | bytes 8224 | tf_op jit(solution)/shard_map/ppermute | solution.py:403
  27.7 0.8 %collective-permute-done.7.uo_ref = f32[4,1024]{1,0:T(4,128)S(1)} collective-permute-done((f32[4,1024]{1,0:T(4,128)S(1)}, f32[4,1024]{1,0:T(4,128)S(1)}, u32[]{:S(2)}, u32[]{:S(2)}) %collective-permute-start.7) | collective-permute-done | bytes 16416 | tf_op jit(solution)/shard_map/ppermute | solution.py:404
  28.5 2.2 %collective-permute-start.9 = (f32[2,1024]{1,0:T(2,128)S(1)}, f32[2,1024]{1,0:T(2,128)S(1)}, u32[]{:S(2)}, u32[]{:S(2)}) collective-permute-start(f32[2,1024]{1,0:T(2,128)S(1)} %slice_add_fusion), channel_id=1, source_target_pairs={{0,8},{16,24},{8,0},{24,16},{1,9},{17,25},{9,1},{25,17},{2,10},{18... | collective-permute-start | bytes 24584 | tf_op jit(solution)/shard_map/ppermute | solution.py:410
  30.7 4.4 %collective-permute-done.9 = f32[2,1024]{1,0:T(2,128)S(1)} collective-permute-done((f32[2,1024]{1,0:T(2,128)S(1)}, f32[2,1024]{1,0:T(2,128)S(1)}, u32[]{:S(2)}, u32[]{:S(2)}) %collective-permute-start.9) | collective-permute-done | bytes 8224 | tf_op jit(solution)/shard_map/ppermute | solution.py:410
  35.1 0.7 %collective-permute-start.11 = (f32[2,1024]{1,0:T(2,128)S(1)}, f32[2,1024]{1,0:T(2,128)S(1)}, u32[]{:S(2)}, u32[]{:S(2)}) collective-permute-start(f32[2,1024]{1,0:T(2,128)S(1)} %add.28), channel_id=1, source_target_pairs={{8,16},{16,8},{9,17},{17,9},{10,18},{18,10},{11,19},{19,11},{12,20... | collective-permute-start | bytes 24584 | tf_op jit(solution)/shard_map/ppermute | solution.py:410
  35.8 1.3 %collective-permute-start.10 = (f32[2,1024]{1,0:T(2,128)S(1)}, f32[2,1024]{1,0:T(2,128)S(1)}, u32[]{:S(2)}, u32[]{:S(2)}) collective-permute-start(f32[2,1024]{1,0:T(2,128)S(1)} %add.28), channel_id=1, source_target_pairs={{16,0},{8,24},{17,1},{9,25},{18,2},{10,26},{19,3},{11,27},{20,4},{... | collective-permute-start | bytes 24584 | tf_op jit(solution)/shard_map/ppermute | solution.py:410
  37.1 0.0 collective-permute-done.11
  37.1 6.1 %collective-permute-done.10 = f32[2,1024]{1,0:T(2,128)S(1)} collective-permute-done((f32[2,1024]{1,0:T(2,128)S(1)}, f32[2,1024]{1,0:T(2,128)S(1)}, u32[]{:S(2)}, u32[]{:S(2)}) %collective-permute-start.10) | collective-permute-done | bytes 8224 | tf_op jit(solution)/shard_map/ppermute | solution.py:410
  43.2 2.1 %collective-permute-start.12 = (f32[2,1024]{1,0:T(2,128)S(1)}, f32[2,1024]{1,0:T(2,128)S(1)}, u32[]{:S(2)}, u32[]{:S(2)}) collective-permute-start(f32[2,1024]{1,0:T(2,128)S(1)} %add_add_fusion), channel_id=1, source_target_pairs={{0,32},{64,96},{128,160},{192,224},{32,0},{96,64},{160,128},{224,1... | collective-permute-start | bytes 24584 | tf_op jit(solution)/shard_map/ppermute | solution.py:410
  45.3 1.6 %collective-permute-done.12 = f32[2,1024]{1,0:T(2,128)S(1)} collective-permute-done((f32[2,1024]{1,0:T(2,128)S(1)}, f32[2,1024]{1,0:T(2,128)S(1)}, u32[]{:S(2)}, u32[]{:S(2)}) %collective-permute-start.12) | collective-permute-done | bytes 8224 | tf_op jit(solution)/shard_map/ppermute | solution.py:410
  47.0 6.8 %collective-permute-start.15 = (f32[2,1024]{1,0:T(2,128)S(1)}, f32[2,1024]{1,0:T(2,128)S(1)}, u32[]{:S(2)}, u32[]{:S(2)}) collective-permute-start(f32[2,1024]{1,0:T(2,128)S(1)} %add.31.refs_0_), channel_id=1, source_target_pairs={{32,64},{96,128},{160,192},{224,0},{64,32},{128,96},{192,160},{0,2... | collective-permute-start | bytes 24584 | tf_op jit(solution)/shard_map/ppermute | solution.py:410
  53.7 1.5 %collective-permute-start.14 = (f32[2,1024]{1,0:T(2,128)S(1)}, f32[2,1024]{1,0:T(2,128)S(1)}, u32[]{:S(2)}, u32[]{:S(2)}) collective-permute-start(f32[2,1024]{1,0:T(2,128)S(1)} %add.31.refs_0_), channel_id=1, source_target_pairs={{0,192},{64,0},{128,64},{192,128},{32,96},{96,160},{160,224},{224,... | collective-permute-start | bytes 24584 | tf_op jit(solution)/shard_map/ppermute | solution.py:410
  55.2 1.0 %collective-permute-start.13 = (f32[2,1024]{1,0:T(2,128)S(1)}, f32[2,1024]{1,0:T(2,128)S(1)}, u32[]{:S(2)}, u32[]{:S(2)}) collective-permute-start(f32[2,1024]{1,0:T(2,128)S(1)} %add.31.refs_0_), channel_id=1, source_target_pairs={{0,160},{32,128},{64,224},{96,192},{160,0},{128,32},{224,64},{192,... | collective-permute-start | bytes 24584 | tf_op jit(solution)/shard_map/ppermute | solution.py:410
  56.2 0.0 collective-permute-done.5.uc_ref
  56.2 0.9 %halo.1 = f32[2,64,1024]{2,1,0:T(8,128)} custom-call(f32[2,64,1024]{2,1,0:T(8,128)S(1)} %get-tuple-element.22.base_ref, f32[2,64,1024]{2,1,0:T(8,128)S(1)} %get-tuple-element.23.wz_ref, f32[4,1024]{1,0:T(4,128)S(1)} %get-tuple-element.24.wy_ref, f32[72,1024]{1,0:T(8,128)S(1)} %collective-permute-done.4.us_ref, f32[64,1024]{1,0:T(8,128)S(1)} %collective-permute-done.5.uc_ref, ...), custom_call_target="tpu_custom_call" | custom-call | flops 1048576 | bytes 2097152 | tf_op jit(solution)/shard_map/halo/pallas_call | solution.py:325
  57.1 0.0 collective-permute-done.15.refs_3_
  57.1 1.2 %collective-permute-done.14.refs_2_ = f32[2,1024]{1,0:T(2,128)S(1)} collective-permute-done((f32[2,1024]{1,0:T(2,128)S(1)}, f32[2,1024]{1,0:T(2,128)S(1)}, u32[]{:S(2)}, u32[]{:S(2)}) %collective-permute-start.14) | collective-permute-done | bytes 8224 | tf_op jit(solution)/shard_map/ppermute | solution.py:410
  58.3 3.6 %collective-permute-done.13.refs_1_ = f32[2,1024]{1,0:T(2,128)S(1)} collective-permute-done((f32[2,1024]{1,0:T(2,128)S(1)}, f32[2,1024]{1,0:T(2,128)S(1)}, u32[]{:S(2)}, u32[]{:S(2)}) %collective-permute-start.13) | collective-permute-done | bytes 8224 | tf_op jit(solution)/shard_map/ppermute | solution.py:410
  61.9 0.8 %scaled.1 = f32[16,128]{1,0:T(8,128)} custom-call(f32[2,1024]{1,0:T(2,128)S(1)} %add.31.refs_0_, f32[2,1024]{1,0:T(2,128)S(1)} %collective-permute-done.13.refs_1_, f32[2,1024]{1,0:T(2,128)S(1)} %collective-permute-done.14.refs_2_, f32[2,1024]{1,0:T(2,128)S(1)} %collective-permute-done.15.refs_3_), custom_call_target="tpu_custom_call" | custom-call | tf_op jit(solution)/shard_map/scaled/pallas_call | solution.py:348
  (9 shorter events, 0.1 us)
Async XLA Ops:
  0.6 7.4 %copy-start.5 = (f32[32]{0:T(128)S(1)}, f32[32]{0:T(128)}, u32[]{:S(2)}) copy-start(f32[32]{0:T(128)} %param.9) | copy-start | bytes 388
  0.6 7.4 %slice-start = ((s8[8388608]{0:T(1024)(128)(4,1)}), s8[4194304]{0:T(1024)(128)(4,1)S(1)}, s32[]{:S(2)}) async-start(s8[8388608]{0:T(1024)(128)(4,1)} %bitcast.4), calls=%async_computation | async-start | bytes 8388608
  0.7 7.4 %copy-start = (f32[2,64,1024]{2,1,0:T(8,128)S(1)}, f32[2,64,1024]{2,1,0:T(8,128)}, u32[]{:S(2)}) copy-start(f32[2,64,1024]{2,1,0:T(8,128)} %iterate_ref.1) | copy-start | bytes 1572868
  0.7 7.4 %slice-start.1 = ((s8[8388608]{0:T(1024)(128)(4,1)}), s8[4194304]{0:T(1024)(128)(4,1)S(1)}, s32[]{:S(2)}) async-start(s8[8388608]{0:T(1024)(128)(4,1)} %bitcast.4), calls=%async_computation.1 | async-start | bytes 8388608
  2.2 9.0 %copy-start.1 = (f32[2,64,1024]{2,1,0:T(8,128)S(1)}, f32[2,64,1024]{2,1,0:T(8,128)}, u32[]{:S(2)}) copy-start(f32[2,64,1024]{2,1,0:T(8,128)} %k_ref.1) | copy-start | bytes 1572868
  2.2 9.0 %copy-start.2 = (f32[2,64,1024]{2,1,0:T(8,128)S(1)}, f32[2,64,1024]{2,1,0:T(8,128)}, u32[]{:S(2)}) copy-start(f32[2,64,1024]{2,1,0:T(8,128)} %rhs_ref.1) | copy-start | bytes 1572868
  2.2 9.0 %copy-start.3 = (s32[2,64,8]{1,2,0:T(8,128)S(1)}, s32[2,64,8]{1,2,0:T(8,128)}, u32[]{:S(2)}) copy-start(s32[2,64,8]{1,2,0:T(8,128)} %param.12) | copy-start | bytes 12292
  2.2 9.0 %copy-start.4 = (s32[2,64,8]{1,2,0:T(8,128)S(1)}, s32[2,64,8]{1,2,0:T(8,128)}, u32[]{:S(2)}) copy-start(s32[2,64,8]{1,2,0:T(8,128)} %param.13) | copy-start | bytes 12292
  2.2 9.0 %collective-permute-start = (f32[72,1024]{1,0:T(8,128)S(1)}, f32[72,1024]{1,0:T(8,128)S(1)}, u32[]{:S(2)}, u32[]{:S(2)}) collective-permute-start(f32[72,1024]{1,0:T(8,128)S(1)} %get-tuple-element.17), channel_id=1, source_target_pairs={{0,4},{8,12},{16,20},{24,28},{32,36},{40,44},{48,52},{56,60},{64,6... | collective-permute-start | bytes 884744 | tf_op jit(solution)/shard_map/ppermute | solution.py:392
  2.3 8.9 %collective-permute-start.1 = (f32[72,1024]{1,0:T(8,128)S(1)}, f32[72,1024]{1,0:T(8,128)S(1)}, u32[]{:S(2)}, u32[]{:S(2)}) collective-permute-start(f32[72,1024]{1,0:T(8,128)S(1)} %get-tuple-element.18), channel_id=1, source_target_pairs={{4,8},{12,16},{20,24},{28,32},{36,40},{44,48},{52,56},{60,64},{68,... | collective-permute-start | bytes 884744 | tf_op jit(solution)/shard_map/ppermute | solution.py:391
  3.2 7.7 %collective-permute-start.2 = (f32[8,1024]{1,0:T(8,128)S(1)}, f32[8,1024]{1,0:T(8,128)S(1)}, u32[]{:S(2)}, u32[]{:S(2)}) collective-permute-start(f32[8,1024]{1,0:T(8,128)S(1)} %get-tuple-element.19), channel_id=1, source_target_pairs={{0,1},{2,3},{1,0},{3,2},{4,5},{6,7},{5,4},{7,6},{8,9},{10,11},{9,8... | collective-permute-start | bytes 98312 | tf_op jit(solution)/shard_map/ppermute | solution.py:393
  5.4 5.8 %collective-permute-start.3 = (f32[8,1024]{1,0:T(8,128)S(1)}, f32[8,1024]{1,0:T(8,128)S(1)}, u32[]{:S(2)}, u32[]{:S(2)}) collective-permute-start(f32[8,1024]{1,0:T(8,128)S(1)} %get-tuple-element.20), channel_id=1, source_target_pairs={{1,2},{2,1},{5,6},{6,5},{9,10},{10,9},{13,14},{14,13},{17,18},{18,... | collective-permute-start | bytes 98312 | tf_op jit(solution)/shard_map/ppermute | solution.py:394
  15.6 3.4 %collective-permute-start.4 = (f32[72,1024]{1,0:T(8,128)S(1)}, f32[72,1024]{1,0:T(8,128)S(1)}, u32[]{:S(2)}, u32[]{:S(2)}) collective-permute-start(f32[72,1024]{1,0:T(8,128)S(1)} %get-tuple-element.25), channel_id=1, source_target_pairs={{0,4},{8,12},{16,20},{24,28},{32,36},{40,44},{48,52},{56,60},{64,6... | collective-permute-start | bytes 884744 | tf_op jit(solution)/shard_map/ppermute | solution.py:398
  19.0 3.8 %collective-permute-start.6 = (f32[4,1024]{1,0:T(4,128)S(1)}, f32[4,1024]{1,0:T(4,128)S(1)}, u32[]{:S(2)}, u32[]{:S(2)}) collective-permute-start(f32[4,1024]{1,0:T(4,128)S(1)} %pad_maximum_fusion), channel_id=1, source_target_pairs={{0,1},{2,3},{1,0},{3,2},{4,5},{6,7},{5,4},{7,6},{8,9},{10,11},{9,8... | collective-permute-start | bytes 49160 | tf_op jit(solution)/shard_map/ppermute | solution.py:401
  22.9 5.6 %collective-permute-start.7 = (f32[4,1024]{1,0:T(4,128)S(1)}, f32[4,1024]{1,0:T(4,128)S(1)}, u32[]{:S(2)}, u32[]{:S(2)}) collective-permute-start(f32[4,1024]{1,0:T(4,128)S(1)} %pad_maximum_fusion.1), channel_id=1, source_target_pairs={{1,2},{2,1},{5,6},{6,5},{9,10},{10,9},{13,14},{14,13},{17,18},{18,... | collective-permute-start | bytes 49160 | tf_op jit(solution)/shard_map/ppermute | solution.py:404
  25.1 2.6 %collective-permute-start.8 = (f32[2,1024]{1,0:T(2,128)S(1)}, f32[2,1024]{1,0:T(2,128)S(1)}, u32[]{:S(2)}, u32[]{:S(2)}) collective-permute-start(f32[2,1024]{1,0:T(2,128)S(1)} %slice_add_fusion.1), channel_id=1, source_target_pairs={{2,0},{1,3},{6,4},{5,7},{10,8},{9,11},{14,12},{13,15},{18,16},{17,... | collective-permute-start | bytes 24584 | tf_op jit(solution)/shard_map/ppermute | solution.py:403
  26.4 29.8 %collective-permute-start.5 = (f32[64,1024]{1,0:T(8,128)S(1)}, f32[64,1024]{1,0:T(8,128)S(1)}, u32[]{:S(2)}, u32[]{:S(2)}) collective-permute-start(f32[64,1024]{1,0:T(8,128)S(1)} %get-tuple-element.26), channel_id=1, source_target_pairs={{4,8},{12,16},{20,24},{28,32},{36,40},{44,48},{52,56},{60,64},{68,... | collective-permute-start | bytes 786440 | tf_op jit(solution)/shard_map/ppermute | solution.py:396
  28.5 6.6 %collective-permute-start.9 = (f32[2,1024]{1,0:T(2,128)S(1)}, f32[2,1024]{1,0:T(2,128)S(1)}, u32[]{:S(2)}, u32[]{:S(2)}) collective-permute-start(f32[2,1024]{1,0:T(2,128)S(1)} %slice_add_fusion), channel_id=1, source_target_pairs={{0,8},{16,24},{8,0},{24,16},{1,9},{17,25},{9,1},{25,17},{2,10},{18... | collective-permute-start | bytes 24584 | tf_op jit(solution)/shard_map/ppermute | solution.py:410
  35.1 2.0 %collective-permute-start.11 = (f32[2,1024]{1,0:T(2,128)S(1)}, f32[2,1024]{1,0:T(2,128)S(1)}, u32[]{:S(2)}, u32[]{:S(2)}) collective-permute-start(f32[2,1024]{1,0:T(2,128)S(1)} %add.28), channel_id=1, source_target_pairs={{8,16},{16,8},{9,17},{17,9},{10,18},{18,10},{11,19},{19,11},{12,20... | collective-permute-start | bytes 24584 | tf_op jit(solution)/shard_map/ppermute | solution.py:410
  35.8 7.4 %collective-permute-start.10 = (f32[2,1024]{1,0:T(2,128)S(1)}, f32[2,1024]{1,0:T(2,128)S(1)}, u32[]{:S(2)}, u32[]{:S(2)}) collective-permute-start(f32[2,1024]{1,0:T(2,128)S(1)} %add.28), channel_id=1, source_target_pairs={{16,0},{8,24},{17,1},{9,25},{18,2},{10,26},{19,3},{11,27},{20,4},{... | collective-permute-start | bytes 24584 | tf_op jit(solution)/shard_map/ppermute | solution.py:410
  43.2 3.8 %collective-permute-start.12 = (f32[2,1024]{1,0:T(2,128)S(1)}, f32[2,1024]{1,0:T(2,128)S(1)}, u32[]{:S(2)}, u32[]{:S(2)}) collective-permute-start(f32[2,1024]{1,0:T(2,128)S(1)} %add_add_fusion), channel_id=1, source_target_pairs={{0,32},{64,96},{128,160},{192,224},{32,0},{96,64},{160,128},{224,1... | collective-permute-start | bytes 24584 | tf_op jit(solution)/shard_map/ppermute | solution.py:410
  47.0 10.2 %collective-permute-start.15 = (f32[2,1024]{1,0:T(2,128)S(1)}, f32[2,1024]{1,0:T(2,128)S(1)}, u32[]{:S(2)}, u32[]{:S(2)}) collective-permute-start(f32[2,1024]{1,0:T(2,128)S(1)} %add.31.refs_0_), channel_id=1, source_target_pairs={{32,64},{96,128},{160,192},{224,0},{64,32},{128,96},{192,160},{0,2... | collective-permute-start | bytes 24584 | tf_op jit(solution)/shard_map/ppermute | solution.py:410
  53.7 4.5 %collective-permute-start.14 = (f32[2,1024]{1,0:T(2,128)S(1)}, f32[2,1024]{1,0:T(2,128)S(1)}, u32[]{:S(2)}, u32[]{:S(2)}) collective-permute-start(f32[2,1024]{1,0:T(2,128)S(1)} %add.31.refs_0_), channel_id=1, source_target_pairs={{0,192},{64,0},{128,64},{192,128},{32,96},{96,160},{160,224},{224,... | collective-permute-start | bytes 24584 | tf_op jit(solution)/shard_map/ppermute | solution.py:410
  55.2 6.7 %collective-permute-start.13 = (f32[2,1024]{1,0:T(2,128)S(1)}, f32[2,1024]{1,0:T(2,128)S(1)}, u32[]{:S(2)}, u32[]{:S(2)}) collective-permute-start(f32[2,1024]{1,0:T(2,128)S(1)} %add.31.refs_0_), channel_id=1, source_target_pairs={{0,160},{32,128},{64,224},{96,192},{160,0},{128,32},{224,64},{192,... | collective-permute-start | bytes 24584 | tf_op jit(solution)/shard_map/ppermute | solution.py:410
where the time goes:
time: 62.9 us; the launch traced here: 62.6 us
  starting transfers between devices  27.6 us (44%)
  waiting for transfers between devices  23.6 us (38%)
  Pallas kernels  10.3 us (16%)
  between operations  0.9 us (1%)
    ppermute x7, waiting for transfers between devices, cycle_end(): lax.ppermute(value, axis, pairs)  16.9 us
    ppermute x7, starting transfers between devices, cycle_end(): lax.ppermute(value, axis, pairs)  15.5 us
    pallas_call x1, Pallas kernels, sketch(): pl.pallas_call(sketch_kernel, out_shape=(field, f32(ny + 8, nx), f32(nz,...  4.39 us
    ppermute x1, waiting for transfers between devices, cycle_end(): u_even = lax.ppermute(jnp.concatenate([value, u_even], 0), 'gy', even)  3.73 us
    pallas_call x1, Pallas kernels, update(): pl.pallas_call(update_kernel, out_shape=(f32(*iterate.shape), f32(*iterat...  2.75 us
    ppermute x1, starting transfers between devices, cycle_end(): k_odd = lax.ppermute(k_odd, 'gy', odd)  2.6 us
    ppermute x1, starting transfers between devices, cycle_end(): k_even = lax.ppermute(k_even, 'gy', even)  2.24 us
    ppermute x1, starting transfers between devices, cycle_end(): u_odd = lax.ppermute(jnp.concatenate([value, u_odd], 0), 'gy', odd)  2.2 us
  transfers between devices with their start and end apart: 16, of which 10 were waited for; matrix products, arithmetic and copies ran while one was open for 0% of the time, Pallas kernels for 6%

commit v1 on v0

--- a/solution.py
+++ b/solution.py
@@ -12,6 +12,8 @@
 SK = 2048
 BLK = 128
 ROWS = SK // BLK
+STEP = 16
+WAYS = BLK // STEP
 GROUP = 4
 GZ = ("z", "x", "core")
 HBM = pl.BlockSpec(memory_space=pltpu.HBM)
@@ -125,17 +127,6 @@
         cost_estimate=pl.CostEstimate(flops=1 << 24, bytes_accessed=2 * basis.size, transcendentals=0),
         name="update",
     )(coeffs.reshape(1, kb), iterate, basis)
-
-
-def lane_gather(values, index):
-    numbers = lax.GatherDimensionNumbers(
-        offset_dims=(),
-        collapsed_slice_dims=(1,),
-        start_index_map=(1,),
-        operand_batching_dims=(0,),
-        start_indices_batching_dims=(0,),
-    )
-    return lax.gather(values, index[..., None], numbers, (1, 1), mode=lax.GatherScatterMode.PROMISE_IN_BOUNDS)
 
 
 def sketch_kernel(
@@ -232,13 +223,15 @@
     sums = []
 
     def place(offs, signs):
-        slot = lax.broadcasted_iota(jnp.int32, (ROWS, offs.shape[1]), 0)
-        return jnp.where(slot == jnp.right_shift(offs, 7), signs, 0.0).astype(jnp.bfloat16)
+        slot = lax.broadcasted_iota(jnp.int32, (WAYS * ROWS, offs.shape[1]), 0)
+        at = (jnp.right_shift(offs, 4) & (WAYS - 1)) * ROWS + jnp.right_shift(offs, 7)
+        return jnp.where(slot == at, signs, 0.0).astype(jnp.bfloat16)
 
     def turn(block, by):
         spot = lax.broadcasted_iota(jnp.int32, block.shape, 1)
         here = spot >= by
-        block = lane_gather(block, (spot - by) & (BLK - 1))
+        for shift in (1, 2, 4, 8):
+            block = jnp.where((by & shift) != 0, pltpu.roll(block, shift, 1), block)
         high = block.astype(jnp.bfloat16)
         low = (block - high.astype(jnp.float32)).astype(jnp.bfloat16)
         none = jnp.zeros_like(high)
@@ -257,7 +250,7 @@
             (base_ref, off_ref[z], mine),
             (hz_ref, theirs[:, :ny].astype(jnp.int32), theirs[:, BLK : BLK + ny]),
         ):
-            turned = columns(offs & (BLK - 1))
+            turned = columns(offs & (STEP - 1))
             for start in range(0, blocks, GROUP):
                 group = range(start, start + GROUP)
                 at = place(
@@ -274,10 +267,13 @@
     for q in range(blocks):
         offs, signs = y_offs[:, lanes(q)], y_signs[:, lanes(q)]
         spots.append(place(jnp.transpose(offs[:, :1]), jnp.transpose(signs[:, :1])))
-        terms.append(turn(hy_ref[:, lanes(q)], offs & (BLK - 1)))
+        terms.append(turn(hy_ref[:, lanes(q)], offs & (STEP - 1)))
     add(spots, terms)
 
-    got = sum(sums[1:], sums[0])
+    wide = sum(sums[1:], sums[0])
+    got = wide[:ROWS]
+    for way in range(1, WAYS):
+        got = got + pltpu.roll(wide[way * ROWS : (way + 1) * ROWS], way * STEP, 1)
     carry = got[:, BLK:]
     part = got[:, :BLK] + jnp.concatenate([carry[ROWS - 1 :], carry[: ROWS - 1]], 0)
     us_ref[ny:, :] = jnp.zeros((8, nx), jnp.float32)
@@ -317,8 +313,8 @@
             rows = slice(y, y + 8)
             value = base_ref[z, rows, :] + wz_ref[z, rows, :] * jnp.where(swap, us_ref[rows, :], uc_ref[rows, :])
             res_ref[z, rows, :] = value
-        res_ref[z, :1, :] += wy_ref[z : z + 1, :] * low_y[nz + z : nz + z + 1, :]
-        res_ref[z, ny - 1 :, :] += wy_ref[nz + z : nz + z + 1, :] * high_y[nz + z : nz + z + 1, :]
+        res_ref[z, :1, :] += wy_ref[z : z + 1, :] * low_y[z : z + 1, :]
+        res_ref[z, ny - 1 :, :] += wy_ref[nz + z : nz + z + 1, :] * high_y[z : z + 1, :]
 
 
 def with_halo(base, *rest):
@@ -368,11 +364,11 @@
     if count == 2:
         return [pairs]
     if count == 4:
-        return [pairs, {"far": [(2, 0), (1, 3)], "near": pairs_from(1, count)}]
+        return [{f"apart{k}": [(i, i ^ k) for i in range(4)] for k in (3, 2, 1)}]
     third = both_ways([(0, 5), (1, 4), (2, 7), (3, 6)])
     second = [(i, (i - 2) % 8) for i in range(0, 8, 2)] + [(i, (i + 2) % 8) for i in range(1, 8, 2)]
     first = both_ways([(i, (i + 1) % 8) for i in range(1, 8, 2)])
-    return [pairs, {"third": third, "second": second, "first": first}]
+    return [pairs, {"apart3": third, "apart2": second, "apart1": first}]
 
 
 def shards(sizes, *arrays):
@@ -393,21 +389,20 @@
     k_even = lax.ppermute(k_even, "gy", even)
     k_odd = lax.ppermute(k_odd, "gy", odd)
     u, u_cross = update(coeffs, iterate, basis)
-    u_cross = lax.ppermute(u_cross, GZ, cross)
     u_out, u_same, u_even, u_odd, base, wz, wy = sketch(u, kappa, rhs, offsets, flips, k_same, k_cross, k_even, k_odd)
     got = lax.ppermute(u_same, GZ, same)
     value = u_same[ny : ny + 2] + got[ny : ny + 2]
     u_same = got
-    u_even = lax.ppermute(jnp.concatenate([value, u_even], 0), "gy", even)
-    value = value + u_even[:2]
-    far = lax.ppermute(value, "gy", rounds(gy)[1]["far"])
-    u_odd = lax.ppermute(jnp.concatenate([value, u_odd], 0), "gy", odd)
-    value = value + far + u_odd[:2]
     terms = [value]
-    for axis in ("x", "z"):
+    for axis in ("gy", "x", "z"):
         for step in rounds(sizes[axis]) if sizes[axis] > 1 else ():
             value = sum(terms[1:], terms[0])
+            if axis == "x":
+                u_cross, value = lax.optimization_barrier((u_cross, value))
             terms = [value] + [lax.ppermute(value, axis, pairs) for pairs in step.values()]
+    u_cross = lax.ppermute(u_cross, GZ, cross)
+    u_even = lax.ppermute(u_even, "gy", even)
+    u_odd = lax.ppermute(u_odd, "gy", odd)
     residual = with_halo(base, wz, wy, u_same, u_cross, u_even, u_odd)
     return u_out, residual, scaled(*terms).reshape(SK)
 

time: 62.9 us -> 64 us (1.017)
  the two profiles are of different devices: /device:TPU:8 before, /device:TPU:40 now
where the time goes in v1:
time: 64 us; the launch traced here: 63.8 us
  starting transfers between devices  32.3 us (50%)
  waiting for transfers between devices  16 us (25%)
  Pallas kernels  14.5 us (23%)
  between operations  0.91 us (1%)
    ppermute x10, starting transfers between devices, cycle_end(): lax.ppermute(value, axis, pairs)  15.8 us
    ppermute x10, waiting for transfers between devices, cycle_end(): lax.ppermute(value, axis, pairs)  14.4 us
    pallas_call x1, Pallas kernels, sketch(): pl.pallas_call(sketch_kernel, out_shape=(field, f32(ny + 8, nx), f32(nz,...  8.58 us
    ppermute x1, starting transfers between devices, cycle_end(): k_cross = lax.ppermute(k_cross, GZ, cross)  4.56 us
    ppermute x1, starting transfers between devices, cycle_end(): k_odd = lax.ppermute(k_odd, 'gy', odd)  4.31 us
    ppermute x1, starting transfers between devices, cycle_end(): u_even = lax.ppermute(u_even, 'gy', even)  3.1 us
    pallas_call x1, Pallas kernels, update(): pl.pallas_call(update_kernel, out_shape=(f32(*iterate.shape), f32(*iterat...  2.75 us
    ppermute x1, starting transfers between devices, cycle_end(): u_cross = lax.ppermute(u_cross, GZ, cross)  1.92 us
  transfers between devices with their start and end apart: 18, of which 8 were waited for; matrix products, arithmetic and copies ran while one was open for 0% of the time, Pallas kernels for 5%

profile of v1, /device:TPU:40, one launch (start us, length us, event | category | flops | bytes accessed | tf_op | source)
XLA Modules:
  0.0 63.8 jit_solution(16071826762631542790)
XLA Ops:
  0.6 0.0 copy-start.5
  0.6 0.0 slice-start
  0.7 0.0 copy-start
  0.7 0.0 slice-start.1
  0.7 1.5 %edges.1 = (f32[72,1024]{1,0:T(8,128)S(1)}, f32[72,1024]{1,0:T(8,128)S(1)}, f32[8,1024]{1,0:T(8,128)S(1)}, f32[8,1024]{1,0:T(8,128)S(1)}) custom-call(f32[2,64,1024]{2,1,0:T(8,128)} %k_ref.1, s32[2,8,64]{2,1,0:T(8,128)} %bitcast.6, s32[2,8,64]{2,1,0:T(8,128)} %bitcast.8), custom_call_target="tpu_custom_call" | custom-call | flops 4294967296 | bytes 268435456 | tf_op jit(solution)/shard_map/edges/pallas_call | solution.py:80
  2.2 0.0 copy-start.1
  2.2 0.0 copy-start.2
  2.2 0.0 copy-start.3
  2.2 0.0 copy-start.4
  2.2 0.1 collective-permute-start
  2.3 4.6 %collective-permute-start.1 = (f32[72,1024]{1,0:T(8,128)S(1)}, f32[72,1024]{1,0:T(8,128)S(1)}, u32[]{:S(2)}, u32[]{:S(2)}) collective-permute-start(f32[72,1024]{1,0:T(8,128)S(1)} %get-tuple-element.20), channel_id=1, source_target_pairs={{4,8},{12,16},{20,24},{28,32},{36,40},{44,48},{52,56},{60,64},{68,... | collective-permute-start | bytes 884744 | tf_op jit(solution)/shard_map/ppermute | solution.py:387
  6.9 0.5 collective-permute-start.2
  7.5 4.3 %collective-permute-start.3 = (f32[8,1024]{1,0:T(8,128)S(1)}, f32[8,1024]{1,0:T(8,128)S(1)}, u32[]{:S(2)}, u32[]{:S(2)}) collective-permute-start(f32[8,1024]{1,0:T(8,128)S(1)} %get-tuple-element.22), channel_id=1, source_target_pairs={{1,2},{2,1},{5,6},{6,5},{9,10},{10,9},{13,14},{14,13},{17,18},{18,... | collective-permute-start | bytes 98312 | tf_op jit(solution)/shard_map/ppermute | solution.py:390
  11.8 0.0 copy-done.5
  11.8 0.0 slice-done
  11.8 0.0 copy-done
  11.8 0.0 slice-done.1
  11.8 2.8 %update.1 = (f32[2,64,1024]{2,1,0:T(8,128)S(1)}, f32[64,1024]{1,0:T(8,128)S(1)}) custom-call(f32[1,32]{1,0:T(1,128)S(1)} %bitcast.10, f32[2,64,1024]{2,1,0:T(8,128)S(1)} %copy-done, bf16[32,2,64,1024]{3,2,1,0:T(8,128)(2,1)S(1)} %bitcast.5), custom_call_target="tpu_custom_call" | custom-call | flops 16777216 | bytes 8388608 | tf_op jit(solution)/shard_map/update/pallas_call | solution.py:120
  14.6 0.0 collective-permute-done.2.even_ref
  14.6 0.0 collective-permute-done.3.odd_ref
  14.6 0.0 collective-permute-done.same_ref
  14.6 0.0 collective-permute-done.1.cross_ref
  14.6 0.0 copy-done.1
  14.6 0.0 copy-done.2
  14.6 0.0 copy-done.3
  14.6 0.0 copy-done.4
  14.7 8.6 %sketch.1 = (f32[2,64,1024]{2,1,0:T(8,128)}, f32[72,1024]{1,0:T(8,128)S(1)}, f32[2,1024]{1,0:T(2,128)S(1)}, f32[2,1024]{1,0:T(2,128)S(1)}, f32[2,64,1024]{2,1,0:...) custom-call(f32[2,64,1024]{2,1,0:T(8,128)S(1)} %get-tuple-element.18.u_ref, ...), custom_call_target="tpu_custom_call" | custom-call | flops 16777216 | bytes 16777216 | tf_op jit(solution)/shard_map/sketch/pallas_call | solution.py:289
  23.2 0.1 collective-permute-start.4
  23.3 1.6 %collective-permute-done.4.us_ref = f32[72,1024]{1,0:T(8,128)S(1)} collective-permute-done((f32[72,1024]{1,0:T(8,128)S(1)}, f32[72,1024]{1,0:T(8,128)S(1)}, u32[]{:S(2)}, u32[]{:S(2)}) %collective-permute-start.4) | collective-permute-done | bytes 294944 | tf_op jit(solution)/shard_map/ppermute | solution.py:393
  24.9 0.0 collective-permute-start.7
  24.9 2.5 %collective-permute-start.6 = (f32[2,1024]{1,0:T(2,128)S(1)}, f32[2,1024]{1,0:T(2,128)S(1)}, u32[]{:S(2)}, u32[]{:S(2)}) collective-permute-start(f32[2,1024]{1,0:T(2,128)S(1)} %slice_add_fusion), channel_id=1, source_target_pairs={{0,2},{1,3},{2,0},{3,1},{4,6},{5,7},{6,4},{7,5},{8,10},{9,11},{10,... | collective-permute-start | bytes 24584 | tf_op jit(solution)/shard_map/ppermute | solution.py:402
  27.4 1.0 %collective-permute-start.5 = (f32[2,1024]{1,0:T(2,128)S(1)}, f32[2,1024]{1,0:T(2,128)S(1)}, u32[]{:S(2)}, u32[]{:S(2)}) collective-permute-start(f32[2,1024]{1,0:T(2,128)S(1)} %slice_add_fusion), channel_id=1, source_target_pairs={{0,3},{1,2},{2,1},{3,0},{4,7},{5,6},{6,5},{7,4},{8,11},{9,10},{10,... | collective-permute-start | bytes 24584 | tf_op jit(solution)/shard_map/ppermute | solution.py:402
  28.4 0.2 collective-permute-done.7
  28.6 1.6 %collective-permute-done.6 = f32[2,1024]{1,0:T(2,128)S(1)} collective-permute-done((f32[2,1024]{1,0:T(2,128)S(1)}, f32[2,1024]{1,0:T(2,128)S(1)}, u32[]{:S(2)}, u32[]{:S(2)}) %collective-permute-start.6) | collective-permute-done | bytes 8224 | tf_op jit(solution)/shard_map/ppermute | solution.py:402
  30.2 0.9 %collective-permute-done.5 = f32[2,1024]{1,0:T(2,128)S(1)} collective-permute-done((f32[2,1024]{1,0:T(2,128)S(1)}, f32[2,1024]{1,0:T(2,128)S(1)}, u32[]{:S(2)}, u32[]{:S(2)}) %collective-permute-start.5) | collective-permute-done | bytes 8224 | tf_op jit(solution)/shard_map/ppermute | solution.py:402
  31.1 1.9 %collective-permute-start.8 = (f32[64,1024]{1,0:T(8,128)S(1)}, f32[64,1024]{1,0:T(8,128)S(1)}, u32[]{:S(2)}, u32[]{:S(2)}) collective-permute-start(f32[64,1024]{1,0:T(8,128)S(1)} %get-tuple-element.29), channel_id=1, source_target_pairs={{4,8},{12,16},{20,24},{28,32},{36,40},{44,48},{52,56},{60,64},{68,... | collective-permute-start | bytes 786440 | tf_op jit(solution)/shard_map/ppermute | solution.py:403
  33.0 0.1 collective-permute-start.13
  33.2 2.9 %collective-permute-start.12 = (f32[2,1024]{1,0:T(2,128)S(1)}, f32[2,1024]{1,0:T(2,128)S(1)}, u32[]{:S(2)}, u32[]{:S(2)}) collective-permute-start(f32[2,1024]{1,0:T(2,128)S(1)} %add_add_fusion.1), channel_id=1, source_target_pairs={{0,16},{8,24},{16,0},{24,8},{1,17},{9,25},{17,1},{25,9},{2,18},{10... | collective-permute-start | bytes 24584 | tf_op jit(solution)/shard_map/ppermute | solution.py:402
  36.1 1.7 %collective-permute-start.11 = (f32[2,1024]{1,0:T(2,128)S(1)}, f32[2,1024]{1,0:T(2,128)S(1)}, u32[]{:S(2)}, u32[]{:S(2)}) collective-permute-start(f32[2,1024]{1,0:T(2,128)S(1)} %add_add_fusion.1), channel_id=1, source_target_pairs={{0,24},{8,16},{16,8},{24,0},{1,25},{9,17},{17,9},{25,1},{2,26},{10... | collective-permute-start | bytes 24584 | tf_op jit(solution)/shard_map/ppermute | solution.py:402
  37.8 0.0 collective-permute-done.13
  37.8 0.7 %collective-permute-done.12 = f32[2,1024]{1,0:T(2,128)S(1)} collective-permute-done((f32[2,1024]{1,0:T(2,128)S(1)}, f32[2,1024]{1,0:T(2,128)S(1)}, u32[]{:S(2)}, u32[]{:S(2)}) %collective-permute-start.12) | collective-permute-done | bytes 8224 | tf_op jit(solution)/shard_map/ppermute | solution.py:402
  38.5 2.6 %collective-permute-done.11 = f32[2,1024]{1,0:T(2,128)S(1)} collective-permute-done((f32[2,1024]{1,0:T(2,128)S(1)}, f32[2,1024]{1,0:T(2,128)S(1)}, u32[]{:S(2)}, u32[]{:S(2)}) %collective-permute-start.11) | collective-permute-done | bytes 8224 | tf_op jit(solution)/shard_map/ppermute | solution.py:402
  41.2 0.1 collective-permute-start.14
  41.3 3.6 %collective-permute-done.14 = f32[2,1024]{1,0:T(2,128)S(1)} collective-permute-done((f32[2,1024]{1,0:T(2,128)S(1)}, f32[2,1024]{1,0:T(2,128)S(1)}, u32[]{:S(2)}, u32[]{:S(2)}) %collective-permute-start.14) | collective-permute-done | bytes 8224 | tf_op jit(solution)/shard_map/ppermute | solution.py:402
  44.9 2.8 %collective-permute-start.17 = (f32[2,1024]{1,0:T(2,128)S(1)}, f32[2,1024]{1,0:T(2,128)S(1)}, u32[]{:S(2)}, u32[]{:S(2)}) collective-permute-start(f32[2,1024]{1,0:T(2,128)S(1)} %add.31.refs_0_), channel_id=1, source_target_pairs={{32,64},{96,128},{160,192},{224,0},{64,32},{128,96},{192,160},{0,2... | collective-permute-start | bytes 24584 | tf_op jit(solution)/shard_map/ppermute | solution.py:402
  47.7 3.1 %collective-permute-start.9 = (f32[2,1024]{1,0:T(2,128)S(1)}, f32[2,1024]{1,0:T(2,128)S(1)}, u32[]{:S(2)}, u32[]{:S(2)}) collective-permute-start(f32[2,1024]{1,0:T(2,128)S(1)} %get-tuple-element.30), channel_id=1, source_target_pairs={{0,1},{2,3},{1,0},{3,2},{4,5},{6,7},{5,4},{7,6},{8,9},{10,11},{9,8... | collective-permute-start | bytes 24584 | tf_op jit(solution)/shard_map/ppermute | solution.py:404
  50.8 4.6 %collective-permute-start.16 = (f32[2,1024]{1,0:T(2,128)S(1)}, f32[2,1024]{1,0:T(2,128)S(1)}, u32[]{:S(2)}, u32[]{:S(2)}) collective-permute-start(f32[2,1024]{1,0:T(2,128)S(1)} %add.31.refs_0_), channel_id=1, source_target_pairs={{0,192},{64,0},{128,64},{192,128},{32,96},{96,160},{160,224},{224,... | collective-permute-start | bytes 24584 | tf_op jit(solution)/shard_map/ppermute | solution.py:402
  55.4 0.0 collective-permute-start.15
  55.4 0.0 collective-permute-done.17.refs_3_
  55.5 1.9 %collective-permute-start.10 = (f32[2,1024]{1,0:T(2,128)S(1)}, f32[2,1024]{1,0:T(2,128)S(1)}, u32[]{:S(2)}, u32[]{:S(2)}) collective-permute-start(f32[2,1024]{1,0:T(2,128)S(1)} %get-tuple-element.31), channel_id=1, source_target_pairs={{1,2},{2,1},{5,6},{6,5},{9,10},{10,9},{13,14},{14,13},{17,18},{18,... | collective-permute-start | bytes 24584 | tf_op jit(solution)/shard_map/ppermute | solution.py:405
  57.4 0.0 collective-permute-done.16.refs_2_
  57.4 4.7 %collective-permute-done.15.refs_1_ = f32[2,1024]{1,0:T(2,128)S(1)} collective-permute-done((f32[2,1024]{1,0:T(2,128)S(1)}, f32[2,1024]{1,0:T(2,128)S(1)}, u32[]{:S(2)}, u32[]{:S(2)}) %collective-permute-start.15) | collective-permute-done | bytes 8224 | tf_op jit(solution)/shard_map/ppermute | solution.py:402
  62.1 0.8 %scaled.1 = f32[16,128]{1,0:T(8,128)} custom-call(f32[2,1024]{1,0:T(2,128)S(1)} %add.31.refs_0_, f32[2,1024]{1,0:T(2,128)S(1)} %collective-permute-done.15.refs_1_, f32[2,1024]{1,0:T(2,128)S(1)} %collective-permute-done.16.refs_2_, f32[2,1024]{1,0:T(2,128)S(1)} %collective-permute-done.17.refs_3_), custom_call_target="tpu_custom_call" | custom-call | tf_op jit(solution)/shard_map/scaled/pallas_call | solution.py:344
  62.9 0.0 collective-permute-done.9.ue_ref
  62.9 0.0 collective-permute-done.10.uo_ref
  62.9 0.0 collective-permute-done.8.uc_ref
  62.9 0.9 %halo.1 = f32[2,64,1024]{2,1,0:T(8,128)} custom-call(f32[2,64,1024]{2,1,0:T(8,128)S(1)} %get-tuple-element.24.base_ref, f32[2,64,1024]{2,1,0:T(8,128)S(1)} %get-tuple-element.25.wz_ref, f32[4,1024]{1,0:T(4,128)S(1)} %get-tuple-element.26.wy_ref, f32[72,1024]{1,0:T(8,128)S(1)} %collective-permute-done.4.us_ref, f32[64,1024]{1,0:T(8,128)S(1)} %collective-permute-done.8.uc_ref, ...), custom_call_target="tpu_custom_call" | custom-call | flops 1048576 | bytes 2097152 | tf_op jit(solution)/shard_map/halo/pallas_call | solution.py:321
  (5 shorter events, 0.0 us)
Async XLA Ops:
  0.6 11.1 %copy-start.5 = (f32[32]{0:T(128)S(1)}, f32[32]{0:T(128)}, u32[]{:S(2)}) copy-start(f32[32]{0:T(128)} %param.9) | copy-start | bytes 388
  0.6 11.1 %slice-start = ((s8[8388608]{0:T(1024)(128)(4,1)}), s8[4194304]{0:T(1024)(128)(4,1)S(1)}, s32[]{:S(2)}) async-start(s8[8388608]{0:T(1024)(128)(4,1)} %bitcast.4), calls=%async_computation | async-start | bytes 8388608
  0.7 11.1 %copy-start = (f32[2,64,1024]{2,1,0:T(8,128)S(1)}, f32[2,64,1024]{2,1,0:T(8,128)}, u32[]{:S(2)}) copy-start(f32[2,64,1024]{2,1,0:T(8,128)} %iterate_ref.1) | copy-start | bytes 1572868
  0.7 11.1 %slice-start.1 = ((s8[8388608]{0:T(1024)(128)(4,1)}), s8[4194304]{0:T(1024)(128)(4,1)S(1)}, s32[]{:S(2)}) async-start(s8[8388608]{0:T(1024)(128)(4,1)} %bitcast.4), calls=%async_computation.1 | async-start | bytes 8388608
  2.2 12.4 %copy-start.1 = (f32[2,64,1024]{2,1,0:T(8,128)S(1)}, f32[2,64,1024]{2,1,0:T(8,128)}, u32[]{:S(2)}) copy-start(f32[2,64,1024]{2,1,0:T(8,128)} %k_ref.1) | copy-start | bytes 1572868
  2.2 12.4 %copy-start.2 = (f32[2,64,1024]{2,1,0:T(8,128)S(1)}, f32[2,64,1024]{2,1,0:T(8,128)}, u32[]{:S(2)}) copy-start(f32[2,64,1024]{2,1,0:T(8,128)} %rhs_ref.1) | copy-start | bytes 1572868
  2.2 12.4 %copy-start.3 = (s32[2,64,8]{1,2,0:T(8,128)S(1)}, s32[2,64,8]{1,2,0:T(8,128)}, u32[]{:S(2)}) copy-start(s32[2,64,8]{1,2,0:T(8,128)} %param.12) | copy-start | bytes 12292
  2.2 12.4 %copy-start.4 = (s32[2,64,8]{1,2,0:T(8,128)S(1)}, s32[2,64,8]{1,2,0:T(8,128)}, u32[]{:S(2)}) copy-start(s32[2,64,8]{1,2,0:T(8,128)} %param.13) | copy-start | bytes 12292
  2.2 12.4 %collective-permute-start = (f32[72,1024]{1,0:T(8,128)S(1)}, f32[72,1024]{1,0:T(8,128)S(1)}, u32[]{:S(2)}, u32[]{:S(2)}) collective-permute-start(f32[72,1024]{1,0:T(8,128)S(1)} %get-tuple-element.19), channel_id=1, source_target_pairs={{0,4},{8,12},{16,20},{24,28},{32,36},{40,44},{48,52},{56,60},{64,6... | collective-permute-start | bytes 884744 | tf_op jit(solution)/shard_map/ppermute | solution.py:388
  2.3 12.3 %collective-permute-start.1 = (f32[72,1024]{1,0:T(8,128)S(1)}, f32[72,1024]{1,0:T(8,128)S(1)}, u32[]{:S(2)}, u32[]{:S(2)}) collective-permute-start(f32[72,1024]{1,0:T(8,128)S(1)} %get-tuple-element.20), channel_id=1, source_target_pairs={{4,8},{12,16},{20,24},{28,32},{36,40},{44,48},{52,56},{60,64},{68,... | collective-permute-start | bytes 884744 | tf_op jit(solution)/shard_map/ppermute | solution.py:387
  6.9 7.7 %collective-permute-start.2 = (f32[8,1024]{1,0:T(8,128)S(1)}, f32[8,1024]{1,0:T(8,128)S(1)}, u32[]{:S(2)}, u32[]{:S(2)}) collective-permute-start(f32[8,1024]{1,0:T(8,128)S(1)} %get-tuple-element.21), channel_id=1, source_target_pairs={{0,1},{2,3},{1,0},{3,2},{4,5},{6,7},{5,4},{7,6},{8,9},{10,11},{9,8... | collective-permute-start | bytes 98312 | tf_op jit(solution)/shard_map/ppermute | solution.py:389
  7.5 7.1 %collective-permute-start.3 = (f32[8,1024]{1,0:T(8,128)S(1)}, f32[8,1024]{1,0:T(8,128)S(1)}, u32[]{:S(2)}, u32[]{:S(2)}) collective-permute-start(f32[8,1024]{1,0:T(8,128)S(1)} %get-tuple-element.22), channel_id=1, source_target_pairs={{1,2},{2,1},{5,6},{6,5},{9,10},{10,9},{13,14},{14,13},{17,18},{18,... | collective-permute-start | bytes 98312 | tf_op jit(solution)/shard_map/ppermute | solution.py:390
  23.2 1.7 %collective-permute-start.4 = (f32[72,1024]{1,0:T(8,128)S(1)}, f32[72,1024]{1,0:T(8,128)S(1)}, u32[]{:S(2)}, u32[]{:S(2)}) collective-permute-start(f32[72,1024]{1,0:T(8,128)S(1)} %get-tuple-element.27), channel_id=1, source_target_pairs={{0,4},{8,12},{16,20},{24,28},{32,36},{40,44},{48,52},{56,60},{64,6... | collective-permute-start | bytes 884744 | tf_op jit(solution)/shard_map/ppermute | solution.py:393
  24.9 3.7 %collective-permute-start.7 = (f32[2,1024]{1,0:T(2,128)S(1)}, f32[2,1024]{1,0:T(2,128)S(1)}, u32[]{:S(2)}, u32[]{:S(2)}) collective-permute-start(f32[2,1024]{1,0:T(2,128)S(1)} %slice_add_fusion), channel_id=1, source_target_pairs={{0,1},{1,0},{2,3},{3,2},{4,5},{5,4},{6,7},{7,6},{8,9},{9,8},{10,11... | collective-permute-start | bytes 24584 | tf_op jit(solution)/shard_map/ppermute | solution.py:402
  24.9 5.2 %collective-permute-start.6 = (f32[2,1024]{1,0:T(2,128)S(1)}, f32[2,1024]{1,0:T(2,128)S(1)}, u32[]{:S(2)}, u32[]{:S(2)}) collective-permute-start(f32[2,1024]{1,0:T(2,128)S(1)} %slice_add_fusion), channel_id=1, source_target_pairs={{0,2},{1,3},{2,0},{3,1},{4,6},{5,7},{6,4},{7,5},{8,10},{9,11},{10,... | collective-permute-start | bytes 24584 | tf_op jit(solution)/shard_map/ppermute | solution.py:402
  27.4 3.7 %collective-permute-start.5 = (f32[2,1024]{1,0:T(2,128)S(1)}, f32[2,1024]{1,0:T(2,128)S(1)}, u32[]{:S(2)}, u32[]{:S(2)}) collective-permute-start(f32[2,1024]{1,0:T(2,128)S(1)} %slice_add_fusion), channel_id=1, source_target_pairs={{0,3},{1,2},{2,1},{3,0},{4,7},{5,6},{6,5},{7,4},{8,11},{9,10},{10,... | collective-permute-start | bytes 24584 | tf_op jit(solution)/shard_map/ppermute | solution.py:402
  31.1 31.8 %collective-permute-start.8 = (f32[64,1024]{1,0:T(8,128)S(1)}, f32[64,1024]{1,0:T(8,128)S(1)}, u32[]{:S(2)}, u32[]{:S(2)}) collective-permute-start(f32[64,1024]{1,0:T(8,128)S(1)} %get-tuple-element.29), channel_id=1, source_target_pairs={{4,8},{12,16},{20,24},{28,32},{36,40},{44,48},{52,56},{60,64},{68,... | collective-permute-start | bytes 786440 | tf_op jit(solution)/shard_map/ppermute | solution.py:403
  33.0 4.8 %collective-permute-start.13 = (f32[2,1024]{1,0:T(2,128)S(1)}, f32[2,1024]{1,0:T(2,128)S(1)}, u32[]{:S(2)}, u32[]{:S(2)}) collective-permute-start(f32[2,1024]{1,0:T(2,128)S(1)} %add_add_fusion.1), channel_id=1, source_target_pairs={{0,8},{8,0},{16,24},{24,16},{1,9},{9,1},{17,25},{25,17},{2,10},{10... | collective-permute-start | bytes 24584 | tf_op jit(solution)/shard_map/ppermute | solution.py:402
  33.2 5.4 %collective-permute-start.12 = (f32[2,1024]{1,0:T(2,128)S(1)}, f32[2,1024]{1,0:T(2,128)S(1)}, u32[]{:S(2)}, u32[]{:S(2)}) collective-permute-start(f32[2,1024]{1,0:T(2,128)S(1)} %add_add_fusion.1), channel_id=1, source_target_pairs={{0,16},{8,24},{16,0},{24,8},{1,17},{9,25},{17,1},{25,9},{2,18},{10... | collective-permute-start | bytes 24584 | tf_op jit(solution)/shard_map/ppermute | solution.py:402
  36.1 5.1 %collective-permute-start.11 = (f32[2,1024]{1,0:T(2,128)S(1)}, f32[2,1024]{1,0:T(2,128)S(1)}, u32[]{:S(2)}, u32[]{:S(2)}) collective-permute-start(f32[2,1024]{1,0:T(2,128)S(1)} %add_add_fusion.1), channel_id=1, source_target_pairs={{0,24},{8,16},{16,8},{24,0},{1,25},{9,17},{17,9},{25,1},{2,26},{10... | collective-permute-start | bytes 24584 | tf_op jit(solution)/shard_map/ppermute | solution.py:402
  41.2 3.7 %collective-permute-start.14 = (f32[2,1024]{1,0:T(2,128)S(1)}, f32[2,1024]{1,0:T(2,128)S(1)}, u32[]{:S(2)}, u32[]{:S(2)}) collective-permute-start(f32[2,1024]{1,0:T(2,128)S(1)} %add_add_fusion), channel_id=1, source_target_pairs={{0,32},{64,96},{128,160},{192,224},{32,0},{96,64},{160,128},{224,1... | collective-permute-start | bytes 24584 | tf_op jit(solution)/shard_map/ppermute | solution.py:402
  44.9 10.5 %collective-permute-start.17 = (f32[2,1024]{1,0:T(2,128)S(1)}, f32[2,1024]{1,0:T(2,128)S(1)}, u32[]{:S(2)}, u32[]{:S(2)}) collective-permute-start(f32[2,1024]{1,0:T(2,128)S(1)} %add.31.refs_0_), channel_id=1, source_target_pairs={{32,64},{96,128},{160,192},{224,0},{64,32},{128,96},{192,160},{0,2... | collective-permute-start | bytes 24584 | tf_op jit(solution)/shard_map/ppermute | solution.py:402
  47.7 15.1 %collective-permute-start.9 = (f32[2,1024]{1,0:T(2,128)S(1)}, f32[2,1024]{1,0:T(2,128)S(1)}, u32[]{:S(2)}, u32[]{:S(2)}) collective-permute-start(f32[2,1024]{1,0:T(2,128)S(1)} %get-tuple-element.30), channel_id=1, source_target_pairs={{0,1},{2,3},{1,0},{3,2},{4,5},{6,7},{5,4},{7,6},{8,9},{10,11},{9,8... | collective-permute-start | bytes 24584 | tf_op jit(solution)/shard_map/ppermute | solution.py:404
  50.8 6.5 %collective-permute-start.16 = (f32[2,1024]{1,0:T(2,128)S(1)}, f32[2,1024]{1,0:T(2,128)S(1)}, u32[]{:S(2)}, u32[]{:S(2)}) collective-permute-start(f32[2,1024]{1,0:T(2,128)S(1)} %add.31.refs_0_), channel_id=1, source_target_pairs={{0,192},{64,0},{128,64},{192,128},{32,96},{96,160},{160,224},{224,... | collective-permute-start | bytes 24584 | tf_op jit(solution)/shard_map/ppermute | solution.py:402
  55.4 6.7 %collective-permute-start.15 = (f32[2,1024]{1,0:T(2,128)S(1)}, f32[2,1024]{1,0:T(2,128)S(1)}, u32[]{:S(2)}, u32[]{:S(2)}) collective-permute-start(f32[2,1024]{1,0:T(2,128)S(1)} %add.31.refs_0_), channel_id=1, source_target_pairs={{0,160},{32,128},{64,224},{96,192},{160,0},{128,32},{224,64},{192,... | collective-permute-start | bytes 24584 | tf_op jit(solution)/shard_map/ppermute | solution.py:402
  55.5 7.4 %collective-permute-start.10 = (f32[2,1024]{1,0:T(2,128)S(1)}, f32[2,1024]{1,0:T(2,128)S(1)}, u32[]{:S(2)}, u32[]{:S(2)}) collective-permute-start(f32[2,1024]{1,0:T(2,128)S(1)} %get-tuple-element.31), channel_id=1, source_target_pairs={{1,2},{2,1},{5,6},{6,5},{9,10},{10,9},{13,14},{14,13},{17,18},{18,... | collective-permute-start | bytes 24584 | tf_op jit(solution)/shard_map/ppermute | solution.py:405

commit v2 on v0

--- a/solution.py
+++ b/solution.py
@@ -30,8 +30,12 @@
     return jnp.transpose(table)
 
 
-def spread(column, q, height):
-    return jnp.broadcast_to(column[:, q : q + 1], (height, BLK))
+def inside():
+    z, x, core, y = (lax.axis_index(a) for a in (*GZ, "gy"))
+    spot = (z * lax.axis_size("x") + x) * 2 + core
+    last = lax.axis_size("z") * lax.axis_size("x") * 2 - 1
+    outer = (spot == 0) | (spot == last), (y == 0) | (y == lax.axis_size("gy") - 1)
+    return [jnp.where(edge, 0.0, 1.0) for edge in outer]
 
 
 def edge_kernel(k_hbm, off_hbm, flip_hbm, same_ref, cross_ref, even_ref, odd_ref, k_ref, off_ref, flip_ref, sems):
@@ -145,6 +149,7 @@
 ):
     nz, ny, nx = u_ref.shape
     core0, even = parities()
+    has_cross, has_odd = inside()
     blocks = nx // BLK
     store = pltpu.make_async_copy(u_ref, out_ref, sem)
     store.start()
@@ -156,8 +161,9 @@
 
     lane = lax.broadcasted_iota(jnp.int32, (8, BLK), 1)
     line = lax.broadcasted_iota(jnp.int32, (8, BLK), 0)
-    low_y = jnp.where(even, odd_ref[...], even_ref[...])
-    high_y = jnp.where(even, even_ref[...], odd_ref[...])
+    odd_lines = odd_ref[...] * has_odd
+    low_y = jnp.where(even, odd_lines, even_ref[...])
+    high_y = jnp.where(even, even_ref[...], odd_lines)
     cells = [(z, q) for z in range(nz) for q in range(blocks)]
 
     def lanes(q):
@@ -191,7 +197,7 @@
             left = None
             for q in range(blocks):
                 c = (z, q)
-                pair = k[c] + jnp.where(swap, same_ref[rows, lanes(q)], cross_ref[rows, lanes(q)])
+                pair = k[c] + jnp.where(swap, same_ref[rows, lanes(q)], cross_ref[rows, lanes(q)] * has_cross)
                 wz = 0.5 * pair
                 wz_ref[z, rows, lanes(q)] = wz
                 hz_ref[z, rows, lanes(q)] = wz * u[c]
@@ -230,6 +236,8 @@
         us_ref[rows, :] = jnp.where(core0, u_ref[1, rows, :], u_ref[0, rows, :])
 
     sums = []
+    block_of = jnp.right_shift(lax.broadcasted_iota(jnp.int32, (blocks, nx), 1), 7)
+    widen = (block_of == lax.broadcasted_iota(jnp.int32, (blocks, nx), 0)).astype(jnp.float32).astype(jnp.bfloat16)
 
     def place(offs, signs):
         slot = lax.broadcasted_iota(jnp.int32, (ROWS, offs.shape[1]), 0)
@@ -251,20 +259,21 @@
 
     for z in range(nz):
         swap = core0 if z else jnp.logical_not(core0)
-        theirs = jnp.where(swap, same_ref[ny:, : 2 * BLK], cross_ref[ny:, : 2 * BLK])
+        theirs = jnp.where(swap, same_ref[ny:, : 2 * BLK], cross_ref[ny:, : 2 * BLK] * has_cross)
         mine = (2 * flip_ref[z] - 1).astype(jnp.float32)
         for source, offs, signs in (
             (base_ref, off_ref[z], mine),
             (hz_ref, theirs[:, :ny].astype(jnp.int32), theirs[:, BLK : BLK + ny]),
         ):
-            turned = columns(offs & (BLK - 1))
+            turned = columns((offs & (BLK - 1)).astype(jnp.float32)).astype(jnp.bfloat16)
+            turned = jnp.dot(turned, widen, preferred_element_type=jnp.float32).astype(jnp.int32)
             for start in range(0, blocks, GROUP):
                 group = range(start, start + GROUP)
                 at = place(
                     jnp.concatenate([offs[q : q + 1, :] for q in group], 1),
                     jnp.concatenate([signs[q : q + 1, :] for q in group], 1),
                 )
-                add([at], [turn(source[z, :, lanes(q)], spread(turned, q, ny)) for q in group])
+                add([at], [turn(source[z, :, lanes(q)], turned[:, lanes(q)]) for q in group])
 
     hy_ref[2 * nz :, :] = jnp.zeros((16 - 2 * nz, nx), jnp.float32)
     unused = jnp.zeros((16 - 2 * nz, nx), jnp.float32)
@@ -309,16 +318,20 @@
 def halo_kernel(base_ref, wz_ref, wy_ref, us_ref, uc_ref, ue_ref, uo_ref, res_ref):
     nz, ny, _ = base_ref.shape
     core0, even = parities()
-    low_y = jnp.where(even, uo_ref[...], ue_ref[...])
-    high_y = jnp.where(even, ue_ref[...], uo_ref[...])
+    has_cross, has_odd = inside()
+    odd_lines = uo_ref[...] * has_odd
+    low_y = jnp.where(even, odd_lines, ue_ref[...])
+    high_y = jnp.where(even, ue_ref[...], odd_lines)
     for z in range(nz):
         swap = core0 if z else jnp.logical_not(core0)
         for y in range(0, ny, 8):
             rows = slice(y, y + 8)
-            value = base_ref[z, rows, :] + wz_ref[z, rows, :] * jnp.where(swap, us_ref[rows, :], uc_ref[rows, :])
+            value = base_ref[z, rows, :] + wz_ref[z, rows, :] * jnp.where(
+                swap, us_ref[rows, :], uc_ref[rows, :] * has_cross
+            )
             res_ref[z, rows, :] = value
-        res_ref[z, :1, :] += wy_ref[z : z + 1, :] * low_y[nz + z : nz + z + 1, :]
-        res_ref[z, ny - 1 :, :] += wy_ref[nz + z : nz + z + 1, :] * high_y[nz + z : nz + z + 1, :]
+        res_ref[z, :1, :] += wy_ref[z : z + 1, :] * low_y[z : z + 1, :]
+        res_ref[z, ny - 1 :, :] += wy_ref[nz + z : nz + z + 1, :] * high_y[z : z + 1, :]
 
 
 def with_halo(base, *rest):
@@ -368,11 +381,11 @@
     if count == 2:
         return [pairs]
     if count == 4:
-        return [pairs, {"far": [(2, 0), (1, 3)], "near": pairs_from(1, count)}]
+        return [{f"apart{k}": [(i, i ^ k) for i in range(4)] for k in (3, 2, 1)}]
     third = both_ways([(0, 5), (1, 4), (2, 7), (3, 6)])
     second = [(i, (i - 2) % 8) for i in range(0, 8, 2)] + [(i, (i + 2) % 8) for i in range(1, 8, 2)]
     first = both_ways([(i, (i + 1) % 8) for i in range(1, 8, 2)])
-    return [pairs, {"third": third, "second": second, "first": first}]
+    return [pairs, {"apart3": third, "apart2": second, "apart1": first}]
 
 
 def shards(sizes, *arrays):
@@ -383,8 +396,8 @@
     gz = sizes["z"] * sizes["x"] * sizes["core"]
     gy = sizes["gy"]
     _, ny, _ = kappa.shape
-    same, cross = pairs_from(0, gz), pairs_from(1, gz)
-    even, odd = pairs_from(0, gy), pairs_from(1, gy)
+    same, cross = pairs_from(0, gz), pairs_from(1, gz) + [(0, 0), (gz - 1, gz - 1)]
+    even, odd = pairs_from(0, gy), pairs_from(1, gy) + [(0, 0), (gy - 1, gy - 1)]
 
     offsets, flips = jnp.swapaxes(offsets, 1, 2), jnp.swapaxes(flips, 1, 2)
     k_same, k_cross, k_even, k_odd = edges(kappa, offsets, flips)
@@ -393,21 +406,20 @@
     k_even = lax.ppermute(k_even, "gy", even)
     k_odd = lax.ppermute(k_odd, "gy", odd)
     u, u_cross = update(coeffs, iterate, basis)
-    u_cross = lax.ppermute(u_cross, GZ, cross)
     u_out, u_same, u_even, u_odd, base, wz, wy = sketch(u, kappa, rhs, offsets, flips, k_same, k_cross, k_even, k_odd)
     got = lax.ppermute(u_same, GZ, same)
     value = u_same[ny : ny + 2] + got[ny : ny + 2]
     u_same = got
-    u_even = lax.ppermute(jnp.concatenate([value, u_even], 0), "gy", even)
-    value = value + u_even[:2]
-    far = lax.ppermute(value, "gy", rounds(gy)[1]["far"])
-    u_odd = lax.ppermute(jnp.concatenate([value, u_odd], 0), "gy", odd)
-    value = value + far + u_odd[:2]
     terms = [value]
-    for axis in ("x", "z"):
+    for axis in ("gy", "x", "z"):
         for step in rounds(sizes[axis]) if sizes[axis] > 1 else ():
             value = sum(terms[1:], terms[0])
+            if axis == "x":
+                u_cross, value = lax.optimization_barrier((u_cross, value))
             terms = [value] + [lax.ppermute(value, axis, pairs) for pairs in step.values()]
+    u_cross = lax.ppermute(u_cross, GZ, cross)
+    u_even = lax.ppermute(u_even, "gy", even)
+    u_odd = lax.ppermute(u_odd, "gy", odd)
     residual = with_halo(base, wz, wy, u_same, u_cross, u_even, u_odd)
     return u_out, residual, scaled(*terms).reshape(SK)
 

time: 62.9 us -> 58.5 us (0.930)
  the two profiles are of different devices: /device:TPU:8 before, /device:TPU:40 now
where the time goes in v2:
time: 58.5 us; the launch traced here: 58.3 us
  starting transfers between devices  32.3 us (55%)
  waiting for transfers between devices  16 us (27%)
  Pallas kernels  9.04 us (15%)
  between operations  0.91 us (2%)
    ppermute x10, starting transfers between devices, cycle_end(): lax.ppermute(value, axis, pairs)  15.8 us
    ppermute x10, waiting for transfers between devices, cycle_end(): lax.ppermute(value, axis, pairs)  14.4 us
    ppermute x1, starting transfers between devices, cycle_end(): k_cross = lax.ppermute(k_cross, GZ, cross)  4.56 us
    ppermute x1, starting transfers between devices, cycle_end(): k_odd = lax.ppermute(k_odd, 'gy', odd)  4.31 us
    ppermute x1, starting transfers between devices, cycle_end(): u_even = lax.ppermute(u_even, 'gy', even)  3.1 us
    pallas_call x1, Pallas kernels, sketch(): pl.pallas_call(sketch_kernel, out_shape=(field, f32(ny + 8, nx), f32(nz,...  3.09 us
    pallas_call x1, Pallas kernels, update(): pl.pallas_call(update_kernel, out_shape=(f32(*iterate.shape), f32(*iterat...  2.75 us
    ppermute x1, starting transfers between devices, cycle_end(): u_cross = lax.ppermute(u_cross, GZ, cross)  1.92 us
  transfers between devices with their start and end apart: 18, of which 8 were waited for; matrix products, arithmetic and copies ran while one was open for 0% of the time, Pallas kernels for 6%

profile of v2, /device:TPU:40, one launch (start us, length us, event | category | flops | bytes accessed | tf_op | source)
XLA Modules:
  0.0 58.3 jit_solution(13348958242464620420)
XLA Ops:
  0.6 0.0 copy-start.5
  0.6 0.0 slice-start
  0.7 0.0 copy-start
  0.7 0.0 slice-start.1
  0.7 1.5 %edges.1 = (f32[72,1024]{1,0:T(8,128)S(1)}, f32[72,1024]{1,0:T(8,128)S(1)}, f32[8,1024]{1,0:T(8,128)S(1)}, f32[8,1024]{1,0:T(8,128)S(1)}) custom-call(f32[2,64,1024]{2,1,0:T(8,128)} %k_ref.1, s32[2,8,64]{2,1,0:T(8,128)} %bitcast.6, s32[2,8,64]{2,1,0:T(8,128)} %bitcast.8), custom_call_target="tpu_custom_call" | custom-call | flops 4294967296 | bytes 268435456 | tf_op jit(solution)/shard_map/edges/pallas_call | solution.py:82
  2.2 0.0 copy-start.1
  2.2 0.0 copy-start.2
  2.2 0.0 copy-start.3
  2.2 0.0 copy-start.4
  2.2 0.1 collective-permute-start
  2.3 4.6 %collective-permute-start.1 = (f32[72,1024]{1,0:T(8,128)S(1)}, f32[72,1024]{1,0:T(8,128)S(1)}, u32[]{:S(2)}, u32[]{:S(2)}) collective-permute-start(f32[72,1024]{1,0:T(8,128)S(1)} %get-tuple-element.20), channel_id=1, source_target_pairs={{4,8},{12,16},{20,24},{28,32},{36,40},{44,48},{52,56},{60,64},{68,... | collective-permute-start | bytes 884744 | tf_op jit(solution)/shard_map/ppermute | solution.py:404
  6.9 0.5 collective-permute-start.2
  7.5 4.3 %collective-permute-start.3 = (f32[8,1024]{1,0:T(8,128)S(1)}, f32[8,1024]{1,0:T(8,128)S(1)}, u32[]{:S(2)}, u32[]{:S(2)}) collective-permute-start(f32[8,1024]{1,0:T(8,128)S(1)} %get-tuple-element.22), channel_id=1, source_target_pairs={{1,2},{2,1},{0,0},{3,3},{5,6},{6,5},{4,4},{7,7},{9,10},{10,9},{8,8... | collective-permute-start | bytes 98312 | tf_op jit(solution)/shard_map/ppermute | solution.py:407
  11.8 0.0 copy-done.5
  11.8 0.0 slice-done
  11.8 0.0 copy-done
  11.8 0.0 slice-done.1
  11.8 2.8 %update.1 = (f32[2,64,1024]{2,1,0:T(8,128)S(1)}, f32[64,1024]{1,0:T(8,128)S(1)}) custom-call(f32[1,32]{1,0:T(1,128)S(1)} %bitcast.10, f32[2,64,1024]{2,1,0:T(8,128)S(1)} %copy-done, bf16[32,2,64,1024]{3,2,1,0:T(8,128)(2,1)S(1)} %bitcast.5), custom_call_target="tpu_custom_call" | custom-call | flops 16777216 | bytes 8388608 | tf_op jit(solution)/shard_map/update/pallas_call | solution.py:122
  14.6 0.0 collective-permute-done.2.even_ref
  14.6 0.0 collective-permute-done.3.odd_ref
  14.6 0.0 collective-permute-done.same_ref
  14.6 0.0 collective-permute-done.1.cross_ref
  14.6 0.0 copy-done.1
  14.6 0.0 copy-done.2
  14.6 0.0 copy-done.3
  14.6 0.0 copy-done.4
  14.7 3.1 %sketch.1 = (f32[2,64,1024]{2,1,0:T(8,128)}, f32[72,1024]{1,0:T(8,128)S(1)}, f32[2,1024]{1,0:T(2,128)S(1)}, f32[2,1024]{1,0:T(2,128)S(1)}, f32[2,64,1024]{2,1,0:...) custom-call(f32[2,64,1024]{2,1,0:T(8,128)S(1)} %get-tuple-element.18.u_ref, ...), custom_call_target="tpu_custom_call" | custom-call | flops 16777216 | bytes 16777216 | tf_op jit(solution)/shard_map/sketch/pallas_call | solution.py:302
  17.8 0.1 collective-permute-start.4
  17.9 1.6 %collective-permute-done.4.us_ref = f32[72,1024]{1,0:T(8,128)S(1)} collective-permute-done((f32[72,1024]{1,0:T(8,128)S(1)}, f32[72,1024]{1,0:T(8,128)S(1)}, u32[]{:S(2)}, u32[]{:S(2)}) %collective-permute-start.4) | collective-permute-done | bytes 294944 | tf_op jit(solution)/shard_map/ppermute | solution.py:410
  19.4 0.0 collective-permute-start.7
  19.4 2.5 %collective-permute-start.6 = (f32[2,1024]{1,0:T(2,128)S(1)}, f32[2,1024]{1,0:T(2,128)S(1)}, u32[]{:S(2)}, u32[]{:S(2)}) collective-permute-start(f32[2,1024]{1,0:T(2,128)S(1)} %slice_add_fusion), channel_id=1, source_target_pairs={{0,2},{1,3},{2,0},{3,1},{4,6},{5,7},{6,4},{7,5},{8,10},{9,11},{10,... | collective-permute-start | bytes 24584 | tf_op jit(solution)/shard_map/ppermute | solution.py:419
  21.9 1.0 %collective-permute-start.5 = (f32[2,1024]{1,0:T(2,128)S(1)}, f32[2,1024]{1,0:T(2,128)S(1)}, u32[]{:S(2)}, u32[]{:S(2)}) collective-permute-start(f32[2,1024]{1,0:T(2,128)S(1)} %slice_add_fusion), channel_id=1, source_target_pairs={{0,3},{1,2},{2,1},{3,0},{4,7},{5,6},{6,5},{7,4},{8,11},{9,10},{10,... | collective-permute-start | bytes 24584 | tf_op jit(solution)/shard_map/ppermute | solution.py:419
  22.9 0.2 collective-permute-done.7
  23.1 1.6 %collective-permute-done.6 = f32[2,1024]{1,0:T(2,128)S(1)} collective-permute-done((f32[2,1024]{1,0:T(2,128)S(1)}, f32[2,1024]{1,0:T(2,128)S(1)}, u32[]{:S(2)}, u32[]{:S(2)}) %collective-permute-start.6) | collective-permute-done | bytes 8224 | tf_op jit(solution)/shard_map/ppermute | solution.py:419
  24.7 0.9 %collective-permute-done.5 = f32[2,1024]{1,0:T(2,128)S(1)} collective-permute-done((f32[2,1024]{1,0:T(2,128)S(1)}, f32[2,1024]{1,0:T(2,128)S(1)}, u32[]{:S(2)}, u32[]{:S(2)}) %collective-permute-start.5) | collective-permute-done | bytes 8224 | tf_op jit(solution)/shard_map/ppermute | solution.py:419
  25.6 1.9 %collective-permute-start.8 = (f32[64,1024]{1,0:T(8,128)S(1)}, f32[64,1024]{1,0:T(8,128)S(1)}, u32[]{:S(2)}, u32[]{:S(2)}) collective-permute-start(f32[64,1024]{1,0:T(8,128)S(1)} %get-tuple-element.29), channel_id=1, source_target_pairs={{4,8},{12,16},{20,24},{28,32},{36,40},{44,48},{52,56},{60,64},{68,... | collective-permute-start | bytes 786440 | tf_op jit(solution)/shard_map/ppermute | solution.py:420
  27.5 0.1 collective-permute-start.13
  27.7 2.9 %collective-permute-start.12 = (f32[2,1024]{1,0:T(2,128)S(1)}, f32[2,1024]{1,0:T(2,128)S(1)}, u32[]{:S(2)}, u32[]{:S(2)}) collective-permute-start(f32[2,1024]{1,0:T(2,128)S(1)} %add_add_fusion.1), channel_id=1, source_target_pairs={{0,16},{8,24},{16,0},{24,8},{1,17},{9,25},{17,1},{25,9},{2,18},{10... | collective-permute-start | bytes 24584 | tf_op jit(solution)/shard_map/ppermute | solution.py:419
  30.6 1.7 %collective-permute-start.11 = (f32[2,1024]{1,0:T(2,128)S(1)}, f32[2,1024]{1,0:T(2,128)S(1)}, u32[]{:S(2)}, u32[]{:S(2)}) collective-permute-start(f32[2,1024]{1,0:T(2,128)S(1)} %add_add_fusion.1), channel_id=1, source_target_pairs={{0,24},{8,16},{16,8},{24,0},{1,25},{9,17},{17,9},{25,1},{2,26},{10... | collective-permute-start | bytes 24584 | tf_op jit(solution)/shard_map/ppermute | solution.py:419
  32.3 0.0 collective-permute-done.13
  32.3 0.7 %collective-permute-done.12 = f32[2,1024]{1,0:T(2,128)S(1)} collective-permute-done((f32[2,1024]{1,0:T(2,128)S(1)}, f32[2,1024]{1,0:T(2,128)S(1)}, u32[]{:S(2)}, u32[]{:S(2)}) %collective-permute-start.12) | collective-permute-done | bytes 8224 | tf_op jit(solution)/shard_map/ppermute | solution.py:419
  33.0 2.6 %collective-permute-done.11 = f32[2,1024]{1,0:T(2,128)S(1)} collective-permute-done((f32[2,1024]{1,0:T(2,128)S(1)}, f32[2,1024]{1,0:T(2,128)S(1)}, u32[]{:S(2)}, u32[]{:S(2)}) %collective-permute-start.11) | collective-permute-done | bytes 8224 | tf_op jit(solution)/shard_map/ppermute | solution.py:419
  35.7 0.1 collective-permute-start.14
  35.8 3.6 %collective-permute-done.14 = f32[2,1024]{1,0:T(2,128)S(1)} collective-permute-done((f32[2,1024]{1,0:T(2,128)S(1)}, f32[2,1024]{1,0:T(2,128)S(1)}, u32[]{:S(2)}, u32[]{:S(2)}) %collective-permute-start.14) | collective-permute-done | bytes 8224 | tf_op jit(solution)/shard_map/ppermute | solution.py:419
  39.4 2.8 %collective-permute-start.17 = (f32[2,1024]{1,0:T(2,128)S(1)}, f32[2,1024]{1,0:T(2,128)S(1)}, u32[]{:S(2)}, u32[]{:S(2)}) collective-permute-start(f32[2,1024]{1,0:T(2,128)S(1)} %add.31.refs_0_), channel_id=1, source_target_pairs={{32,64},{96,128},{160,192},{224,0},{64,32},{128,96},{192,160},{0,2... | collective-permute-start | bytes 24584 | tf_op jit(solution)/shard_map/ppermute | solution.py:419
  42.3 3.1 %collective-permute-start.9 = (f32[2,1024]{1,0:T(2,128)S(1)}, f32[2,1024]{1,0:T(2,128)S(1)}, u32[]{:S(2)}, u32[]{:S(2)}) collective-permute-start(f32[2,1024]{1,0:T(2,128)S(1)} %get-tuple-element.30), channel_id=1, source_target_pairs={{0,1},{2,3},{1,0},{3,2},{4,5},{6,7},{5,4},{7,6},{8,9},{10,11},{9,8... | collective-permute-start | bytes 24584 | tf_op jit(solution)/shard_map/ppermute | solution.py:421
  45.4 4.6 %collective-permute-start.16 = (f32[2,1024]{1,0:T(2,128)S(1)}, f32[2,1024]{1,0:T(2,128)S(1)}, u32[]{:S(2)}, u32[]{:S(2)}) collective-permute-start(f32[2,1024]{1,0:T(2,128)S(1)} %add.31.refs_0_), channel_id=1, source_target_pairs={{0,192},{64,0},{128,64},{192,128},{32,96},{96,160},{160,224},{224,... | collective-permute-start | bytes 24584 | tf_op jit(solution)/shard_map/ppermute | solution.py:419
  50.0 0.0 collective-permute-start.15
  50.0 0.0 collective-permute-done.17.refs_3_
  50.0 1.9 %collective-permute-start.10 = (f32[2,1024]{1,0:T(2,128)S(1)}, f32[2,1024]{1,0:T(2,128)S(1)}, u32[]{:S(2)}, u32[]{:S(2)}) collective-permute-start(f32[2,1024]{1,0:T(2,128)S(1)} %get-tuple-element.31), channel_id=1, source_target_pairs={{1,2},{2,1},{0,0},{3,3},{5,6},{6,5},{4,4},{7,7},{9,10},{10,9},{8,8... | collective-permute-start | bytes 24584 | tf_op jit(solution)/shard_map/ppermute | solution.py:422
  51.9 0.0 collective-permute-done.16.refs_2_
  51.9 4.7 %collective-permute-done.15.refs_1_ = f32[2,1024]{1,0:T(2,128)S(1)} collective-permute-done((f32[2,1024]{1,0:T(2,128)S(1)}, f32[2,1024]{1,0:T(2,128)S(1)}, u32[]{:S(2)}, u32[]{:S(2)}) %collective-permute-start.15) | collective-permute-done | bytes 8224 | tf_op jit(solution)/shard_map/ppermute | solution.py:419
  56.6 0.8 %scaled.1 = f32[16,128]{1,0:T(8,128)} custom-call(f32[2,1024]{1,0:T(2,128)S(1)} %add.31.refs_0_, f32[2,1024]{1,0:T(2,128)S(1)} %collective-permute-done.15.refs_1_, f32[2,1024]{1,0:T(2,128)S(1)} %collective-permute-done.16.refs_2_, f32[2,1024]{1,0:T(2,128)S(1)} %collective-permute-done.17.refs_3_), custom_call_target="tpu_custom_call" | custom-call | tf_op jit(solution)/shard_map/scaled/pallas_call | solution.py:361
  57.4 0.0 collective-permute-done.9.ue_ref
  57.4 0.0 collective-permute-done.10.uo_ref
  57.4 0.0 collective-permute-done.8.uc_ref
  57.4 0.9 %halo.1 = f32[2,64,1024]{2,1,0:T(8,128)} custom-call(f32[2,64,1024]{2,1,0:T(8,128)S(1)} %get-tuple-element.24.base_ref, f32[2,64,1024]{2,1,0:T(8,128)S(1)} %get-tuple-element.25.wz_ref, f32[4,1024]{1,0:T(4,128)S(1)} %get-tuple-element.26.wy_ref, f32[72,1024]{1,0:T(8,128)S(1)} %collective-permute-done.4.us_ref, f32[64,1024]{1,0:T(8,128)S(1)} %collective-permute-done.8.uc_ref, ...), custom_call_target="tpu_custom_call" | custom-call | flops 1048576 | bytes 2097152 | tf_op jit(solution)/shard_map/halo/pallas_call | solution.py:338
  (5 shorter events, 0.0 us)
Async XLA Ops:
  0.6 11.1 %copy-start.5 = (f32[32]{0:T(128)S(1)}, f32[32]{0:T(128)}, u32[]{:S(2)}) copy-start(f32[32]{0:T(128)} %param.9) | copy-start | bytes 388
  0.6 11.1 %slice-start = ((s8[8388608]{0:T(1024)(128)(4,1)}), s8[4194304]{0:T(1024)(128)(4,1)S(1)}, s32[]{:S(2)}) async-start(s8[8388608]{0:T(1024)(128)(4,1)} %bitcast.4), calls=%async_computation | async-start | bytes 8388608
  0.7 11.1 %copy-start = (f32[2,64,1024]{2,1,0:T(8,128)S(1)}, f32[2,64,1024]{2,1,0:T(8,128)}, u32[]{:S(2)}) copy-start(f32[2,64,1024]{2,1,0:T(8,128)} %iterate_ref.1) | copy-start | bytes 1572868
  0.7 11.1 %slice-start.1 = ((s8[8388608]{0:T(1024)(128)(4,1)}), s8[4194304]{0:T(1024)(128)(4,1)S(1)}, s32[]{:S(2)}) async-start(s8[8388608]{0:T(1024)(128)(4,1)} %bitcast.4), calls=%async_computation.1 | async-start | bytes 8388608
  2.2 12.4 %copy-start.1 = (f32[2,64,1024]{2,1,0:T(8,128)S(1)}, f32[2,64,1024]{2,1,0:T(8,128)}, u32[]{:S(2)}) copy-start(f32[2,64,1024]{2,1,0:T(8,128)} %k_ref.1) | copy-start | bytes 1572868
  2.2 12.4 %copy-start.2 = (f32[2,64,1024]{2,1,0:T(8,128)S(1)}, f32[2,64,1024]{2,1,0:T(8,128)}, u32[]{:S(2)}) copy-start(f32[2,64,1024]{2,1,0:T(8,128)} %rhs_ref.1) | copy-start | bytes 1572868
  2.2 12.4 %copy-start.3 = (s32[2,64,8]{1,2,0:T(8,128)S(1)}, s32[2,64,8]{1,2,0:T(8,128)}, u32[]{:S(2)}) copy-start(s32[2,64,8]{1,2,0:T(8,128)} %param.12) | copy-start | bytes 12292
  2.2 12.4 %copy-start.4 = (s32[2,64,8]{1,2,0:T(8,128)S(1)}, s32[2,64,8]{1,2,0:T(8,128)}, u32[]{:S(2)}) copy-start(s32[2,64,8]{1,2,0:T(8,128)} %param.13) | copy-start | bytes 12292
  2.2 12.4 %collective-permute-start = (f32[72,1024]{1,0:T(8,128)S(1)}, f32[72,1024]{1,0:T(8,128)S(1)}, u32[]{:S(2)}, u32[]{:S(2)}) collective-permute-start(f32[72,1024]{1,0:T(8,128)S(1)} %get-tuple-element.19), channel_id=1, source_target_pairs={{0,4},{8,12},{16,20},{24,28},{32,36},{40,44},{48,52},{56,60},{64,6... | collective-permute-start | bytes 884744 | tf_op jit(solution)/shard_map/ppermute | solution.py:405
  2.3 12.3 %collective-permute-start.1 = (f32[72,1024]{1,0:T(8,128)S(1)}, f32[72,1024]{1,0:T(8,128)S(1)}, u32[]{:S(2)}, u32[]{:S(2)}) collective-permute-start(f32[72,1024]{1,0:T(8,128)S(1)} %get-tuple-element.20), channel_id=1, source_target_pairs={{4,8},{12,16},{20,24},{28,32},{36,40},{44,48},{52,56},{60,64},{68,... | collective-permute-start | bytes 884744 | tf_op jit(solution)/shard_map/ppermute | solution.py:404
  6.9 7.7 %collective-permute-start.2 = (f32[8,1024]{1,0:T(8,128)S(1)}, f32[8,1024]{1,0:T(8,128)S(1)}, u32[]{:S(2)}, u32[]{:S(2)}) collective-permute-start(f32[8,1024]{1,0:T(8,128)S(1)} %get-tuple-element.21), channel_id=1, source_target_pairs={{0,1},{2,3},{1,0},{3,2},{4,5},{6,7},{5,4},{7,6},{8,9},{10,11},{9,8... | collective-permute-start | bytes 98312 | tf_op jit(solution)/shard_map/ppermute | solution.py:406
  7.5 7.1 %collective-permute-start.3 = (f32[8,1024]{1,0:T(8,128)S(1)}, f32[8,1024]{1,0:T(8,128)S(1)}, u32[]{:S(2)}, u32[]{:S(2)}) collective-permute-start(f32[8,1024]{1,0:T(8,128)S(1)} %get-tuple-element.22), channel_id=1, source_target_pairs={{1,2},{2,1},{0,0},{3,3},{5,6},{6,5},{4,4},{7,7},{9,10},{10,9},{8,8... | collective-permute-start | bytes 98312 | tf_op jit(solution)/shard_map/ppermute | solution.py:407
  17.8 1.7 %collective-permute-start.4 = (f32[72,1024]{1,0:T(8,128)S(1)}, f32[72,1024]{1,0:T(8,128)S(1)}, u32[]{:S(2)}, u32[]{:S(2)}) collective-permute-start(f32[72,1024]{1,0:T(8,128)S(1)} %get-tuple-element.27), channel_id=1, source_target_pairs={{0,4},{8,12},{16,20},{24,28},{32,36},{40,44},{48,52},{56,60},{64,6... | collective-permute-start | bytes 884744 | tf_op jit(solution)/shard_map/ppermute | solution.py:410
  19.4 3.7 %collective-permute-start.7 = (f32[2,1024]{1,0:T(2,128)S(1)}, f32[2,1024]{1,0:T(2,128)S(1)}, u32[]{:S(2)}, u32[]{:S(2)}) collective-permute-start(f32[2,1024]{1,0:T(2,128)S(1)} %slice_add_fusion), channel_id=1, source_target_pairs={{0,1},{1,0},{2,3},{3,2},{4,5},{5,4},{6,7},{7,6},{8,9},{9,8},{10,11... | collective-permute-start | bytes 24584 | tf_op jit(solution)/shard_map/ppermute | solution.py:419
  19.4 5.2 %collective-permute-start.6 = (f32[2,1024]{1,0:T(2,128)S(1)}, f32[2,1024]{1,0:T(2,128)S(1)}, u32[]{:S(2)}, u32[]{:S(2)}) collective-permute-start(f32[2,1024]{1,0:T(2,128)S(1)} %slice_add_fusion), channel_id=1, source_target_pairs={{0,2},{1,3},{2,0},{3,1},{4,6},{5,7},{6,4},{7,5},{8,10},{9,11},{10,... | collective-permute-start | bytes 24584 | tf_op jit(solution)/shard_map/ppermute | solution.py:419
  21.9 3.7 %collective-permute-start.5 = (f32[2,1024]{1,0:T(2,128)S(1)}, f32[2,1024]{1,0:T(2,128)S(1)}, u32[]{:S(2)}, u32[]{:S(2)}) collective-permute-start(f32[2,1024]{1,0:T(2,128)S(1)} %slice_add_fusion), channel_id=1, source_target_pairs={{0,3},{1,2},{2,1},{3,0},{4,7},{5,6},{6,5},{7,4},{8,11},{9,10},{10,... | collective-permute-start | bytes 24584 | tf_op jit(solution)/shard_map/ppermute | solution.py:419
  25.6 31.8 %collective-permute-start.8 = (f32[64,1024]{1,0:T(8,128)S(1)}, f32[64,1024]{1,0:T(8,128)S(1)}, u32[]{:S(2)}, u32[]{:S(2)}) collective-permute-start(f32[64,1024]{1,0:T(8,128)S(1)} %get-tuple-element.29), channel_id=1, source_target_pairs={{4,8},{12,16},{20,24},{28,32},{36,40},{44,48},{52,56},{60,64},{68,... | collective-permute-start | bytes 786440 | tf_op jit(solution)/shard_map/ppermute | solution.py:420
  27.5 4.8 %collective-permute-start.13 = (f32[2,1024]{1,0:T(2,128)S(1)}, f32[2,1024]{1,0:T(2,128)S(1)}, u32[]{:S(2)}, u32[]{:S(2)}) collective-permute-start(f32[2,1024]{1,0:T(2,128)S(1)} %add_add_fusion.1), channel_id=1, source_target_pairs={{0,8},{8,0},{16,24},{24,16},{1,9},{9,1},{17,25},{25,17},{2,10},{10... | collective-permute-start | bytes 24584 | tf_op jit(solution)/shard_map/ppermute | solution.py:419
  27.7 5.4 %collective-permute-start.12 = (f32[2,1024]{1,0:T(2,128)S(1)}, f32[2,1024]{1,0:T(2,128)S(1)}, u32[]{:S(2)}, u32[]{:S(2)}) collective-permute-start(f32[2,1024]{1,0:T(2,128)S(1)} %add_add_fusion.1), channel_id=1, source_target_pairs={{0,16},{8,24},{16,0},{24,8},{1,17},{9,25},{17,1},{25,9},{2,18},{10... | collective-permute-start | bytes 24584 | tf_op jit(solution)/shard_map/ppermute | solution.py:419
  30.6 5.1 %collective-permute-start.11 = (f32[2,1024]{1,0:T(2,128)S(1)}, f32[2,1024]{1,0:T(2,128)S(1)}, u32[]{:S(2)}, u32[]{:S(2)}) collective-permute-start(f32[2,1024]{1,0:T(2,128)S(1)} %add_add_fusion.1), channel_id=1, source_target_pairs={{0,24},{8,16},{16,8},{24,0},{1,25},{9,17},{17,9},{25,1},{2,26},{10... | collective-permute-start | bytes 24584 | tf_op jit(solution)/shard_map/ppermute | solution.py:419
  35.7 3.7 %collective-permute-start.14 = (f32[2,1024]{1,0:T(2,128)S(1)}, f32[2,1024]{1,0:T(2,128)S(1)}, u32[]{:S(2)}, u32[]{:S(2)}) collective-permute-start(f32[2,1024]{1,0:T(2,128)S(1)} %add_add_fusion), channel_id=1, source_target_pairs={{0,32},{64,96},{128,160},{192,224},{32,0},{96,64},{160,128},{224,1... | collective-permute-start | bytes 24584 | tf_op jit(solution)/shard_map/ppermute | solution.py:419
  39.4 10.5 %collective-permute-start.17 = (f32[2,1024]{1,0:T(2,128)S(1)}, f32[2,1024]{1,0:T(2,128)S(1)}, u32[]{:S(2)}, u32[]{:S(2)}) collective-permute-start(f32[2,1024]{1,0:T(2,128)S(1)} %add.31.refs_0_), channel_id=1, source_target_pairs={{32,64},{96,128},{160,192},{224,0},{64,32},{128,96},{192,160},{0,2... | collective-permute-start | bytes 24584 | tf_op jit(solution)/shard_map/ppermute | solution.py:419
  42.3 15.1 %collective-permute-start.9 = (f32[2,1024]{1,0:T(2,128)S(1)}, f32[2,1024]{1,0:T(2,128)S(1)}, u32[]{:S(2)}, u32[]{:S(2)}) collective-permute-start(f32[2,1024]{1,0:T(2,128)S(1)} %get-tuple-element.30), channel_id=1, source_target_pairs={{0,1},{2,3},{1,0},{3,2},{4,5},{6,7},{5,4},{7,6},{8,9},{10,11},{9,8... | collective-permute-start | bytes 24584 | tf_op jit(solution)/shard_map/ppermute | solution.py:421
  45.4 6.5 %collective-permute-start.16 = (f32[2,1024]{1,0:T(2,128)S(1)}, f32[2,1024]{1,0:T(2,128)S(1)}, u32[]{:S(2)}, u32[]{:S(2)}) collective-permute-start(f32[2,1024]{1,0:T(2,128)S(1)} %add.31.refs_0_), channel_id=1, source_target_pairs={{0,192},{64,0},{128,64},{192,128},{32,96},{96,160},{160,224},{224,... | collective-permute-start | bytes 24584 | tf_op jit(solution)/shard_map/ppermute | solution.py:419
  50.0 6.7 %collective-permute-start.15 = (f32[2,1024]{1,0:T(2,128)S(1)}, f32[2,1024]{1,0:T(2,128)S(1)}, u32[]{:S(2)}, u32[]{:S(2)}) collective-permute-start(f32[2,1024]{1,0:T(2,128)S(1)} %add.31.refs_0_), channel_id=1, source_target_pairs={{0,160},{32,128},{64,224},{96,192},{160,0},{128,32},{224,64},{192,... | collective-permute-start | bytes 24584 | tf_op jit(solution)/shard_map/ppermute | solution.py:419
  50.0 7.4 %collective-permute-start.10 = (f32[2,1024]{1,0:T(2,128)S(1)}, f32[2,1024]{1,0:T(2,128)S(1)}, u32[]{:S(2)}, u32[]{:S(2)}) collective-permute-start(f32[2,1024]{1,0:T(2,128)S(1)} %get-tuple-element.31), channel_id=1, source_target_pairs={{1,2},{2,1},{0,0},{3,3},{5,6},{6,5},{4,4},{7,7},{9,10},{10,9},{8,8... | collective-permute-start | bytes 24584 | tf_op jit(solution)/shard_map/ppermute | solution.py:422

commit v3 on v2

--- a/solution.py
+++ b/solution.py
@@ -91,44 +91,55 @@
     )(*(pltpu.with_memory_space_constraint(v, pltpu.HBM) for v in (kappa, offsets, flips)))
 
 
-def update_kernel(coeff_ref, iterate_ref, basis_ref, u_ref, uc_ref, splat):
-    kb, nz, ny, nx = basis_ref.shape
+def update_kernel(coeff_ref, iterate_ref, basis_ref, u_ref, us_ref, uc_ref, splat):
+    kb, nz, ny, _ = basis_ref.shape
     core0, _ = parities()
     rounded = coeff_ref[...].astype(jnp.bfloat16).astype(jnp.float32)
     for k in range(kb):
         splat[k] = jnp.broadcast_to(rounded[:, k : k + 1], (8, BLK))
 
-    @pl.loop(0, ny // 16)
+    @pl.loop(0, ny // 32)
     def _(i):
-        rows = pl.ds(pl.multiple_of(i * 16, 16), 16)
-
-        @pl.loop(0, nx // (2 * BLK))
-        def _(j):
-            lanes = [pl.ds(pl.multiple_of((2 * j + h) * BLK, BLK), BLK) for h in range(2)]
-            spots = [(z, rows, part) for z in range(nz) for part in lanes]
-            acc = [iterate_ref[spot] for spot in spots]
-            for k in range(kb):
-                scale = jnp.concatenate([splat[k]] * 2, 0)
-                for n, spot in enumerate(spots):
-                    acc[n] = acc[n] + scale * basis_ref[(k, *spot)].astype(jnp.float32)
+        rows = [pl.ds(pl.multiple_of(i * 32 + 16 * h, 16), 16) for h in range(2)]
+        spots = [(z, part, slice(None)) for z in range(nz) for part in rows]
+        acc = [iterate_ref[spot] for spot in spots]
+        for k in range(kb):
+            scale = jnp.concatenate([splat[k]] * 2, 0)
             for n, spot in enumerate(spots):
-                u_ref[spot] = acc[n]
-            for n, part in enumerate(lanes):
-                uc_ref[rows, part] = jnp.where(core0, acc[n], acc[len(lanes) + n])
+                acc[n] = acc[n] + scale * basis_ref[(k, *spot)].astype(jnp.float32)
+        for n, spot in enumerate(spots):
+            u_ref[spot] = acc[n]
+        for n, part in enumerate(rows):
+            us_ref[part] = jnp.where(core0, acc[len(rows) + n], acc[n])
+            uc_ref[part] = jnp.where(core0, acc[n], acc[len(rows) + n])
+
+
+def tiled(value):
+    *lead, ny, nx = value.shape
+    value = jnp.swapaxes(value.reshape(*lead, ny // 8, 8, nx // BLK, BLK), -3, -2)
+    return value.reshape(*lead, ny * nx // BLK, BLK)
+
+
+def untiled(value, nx):
+    *lead, rows, _ = value.shape
+    value = jnp.swapaxes(value.reshape(*lead, rows * BLK // (8 * nx), nx // BLK, 8, BLK), -3, -2)
+    return value.reshape(*lead, rows * BLK // nx, nx)
 
 
 def update(coeffs, iterate, basis):
-    kb = basis.shape[0]
-    return pl.pallas_call(
+    kb, nx = basis.shape[0], basis.shape[3]
+    iterate, basis = tiled(iterate), tiled(basis)
+    values = pl.pallas_call(
         update_kernel,
-        out_shape=(f32(*iterate.shape), f32(*iterate.shape[1:])),
+        out_shape=(f32(*iterate.shape), f32(*iterate.shape[1:]), f32(*iterate.shape[1:])),
         in_specs=[VMEM] * 3,
-        out_specs=(VMEM, VMEM),
+        out_specs=(VMEM,) * 3,
         scratch_shapes=[pltpu.VMEM((kb, 8, BLK), jnp.float32)],
         compiler_params=pltpu.CompilerParams(vmem_limit_bytes=16 << 20),
         cost_estimate=pl.CostEstimate(flops=1 << 24, bytes_accessed=2 * basis.size, transcendentals=0),
         name="update",
     )(coeffs.reshape(1, kb), iterate, basis)
+    return [untiled(value, nx) for value in values]
 
 
 def lane_gather(values, index):
@@ -144,7 +155,7 @@
 
 def sketch_kernel(
     u_ref, k_ref, rhs_ref, off_ref, flip_ref, same_ref, cross_ref, even_ref, odd_ref,
-    out_ref, us_ref, ue_ref, uo_ref, base_ref, wz_ref, wy_ref,
+    out_ref, ue_ref, uo_ref, base_ref, wz_ref, wy_ref, part_ref,
     hz_ref, hy_ref, sem,
 ):
     nz, ny, nx = u_ref.shape
@@ -231,10 +242,6 @@
         below = above
         u, k, u_up, k_up = u_next, k_next, u_next_up, k_next_up
 
-    for y in range(0, ny, 8):
-        rows = slice(y, y + 8)
-        us_ref[rows, :] = jnp.where(core0, u_ref[1, rows, :], u_ref[0, rows, :])
-
     sums = []
     block_of = jnp.right_shift(lax.broadcasted_iota(jnp.int32, (blocks, nx), 1), 7)
     widen = (block_of == lax.broadcasted_iota(jnp.int32, (blocks, nx), 0)).astype(jnp.float32).astype(jnp.bfloat16)
@@ -289,10 +296,8 @@
     got = sum(sums[1:], sums[0])
     carry = got[:, BLK:]
     part = got[:, :BLK] + jnp.concatenate([carry[ROWS - 1 :], carry[: ROWS - 1]], 0)
-    us_ref[ny:, :] = jnp.zeros((8, nx), jnp.float32)
     for m in range(ROWS):
-        at = ny + m // blocks
-        us_ref[at : at + 1, lanes(m % blocks)] = part[m : m + 1]
+        part_ref[m // blocks : m // blocks + 1, lanes(m % blocks)] = part[m : m + 1]
     store.wait()
 
 
@@ -301,7 +306,9 @@
     field = f32(nz, ny, nx)
     return pl.pallas_call(
         sketch_kernel,
-        out_shape=(field, f32(ny + 8, nx), f32(nz, nx), f32(nz, nx), field, field, f32(2 * nz, nx)),
+        out_shape=(
+            field, f32(nz, nx), f32(nz, nx), field, field, f32(2 * nz, nx), f32(SK // nx, nx),
+        ),
         in_specs=[VMEM] * 9,
         out_specs=(pl.BlockSpec(memory_space=pl.ANY),) + (VMEM,) * 6,
         scratch_shapes=[
@@ -395,7 +402,6 @@
 def cycle_end(sizes, iterate, basis, coeffs, rhs, kappa, offsets, flips):
     gz = sizes["z"] * sizes["x"] * sizes["core"]
     gy = sizes["gy"]
-    _, ny, _ = kappa.shape
     same, cross = pairs_from(0, gz), pairs_from(1, gz) + [(0, 0), (gz - 1, gz - 1)]
     even, odd = pairs_from(0, gy), pairs_from(1, gy) + [(0, 0), (gy - 1, gy - 1)]
 
@@ -405,11 +411,12 @@
     k_same = lax.ppermute(k_same, GZ, same)
     k_even = lax.ppermute(k_even, "gy", even)
     k_odd = lax.ppermute(k_odd, "gy", odd)
-    u, u_cross = update(coeffs, iterate, basis)
-    u_out, u_same, u_even, u_odd, base, wz, wy = sketch(u, kappa, rhs, offsets, flips, k_same, k_cross, k_even, k_odd)
-    got = lax.ppermute(u_same, GZ, same)
-    value = u_same[ny : ny + 2] + got[ny : ny + 2]
-    u_same = got
+    u, u_same, u_cross = update(coeffs, iterate, basis)
+    u_out, u_even, u_odd, base, wz, wy, part = sketch(
+        u, kappa, rhs, offsets, flips, k_same, k_cross, k_even, k_odd
+    )
+    u_same, part = lax.optimization_barrier((u_same, part))
+    value = part + lax.ppermute(part, GZ, same)
     terms = [value]
     for axis in ("gy", "x", "z"):
         for step in rounds(sizes[axis]) if sizes[axis] > 1 else ():
@@ -418,6 +425,7 @@
                 u_cross, value = lax.optimization_barrier((u_cross, value))
             terms = [value] + [lax.ppermute(value, axis, pairs) for pairs in step.values()]
     u_cross = lax.ppermute(u_cross, GZ, cross)
+    u_same = lax.ppermute(u_same, GZ, same)
     u_even = lax.ppermute(u_even, "gy", even)
     u_odd = lax.ppermute(u_odd, "gy", odd)
     residual = with_halo(base, wz, wy, u_same, u_cross, u_even, u_odd)

time: 58.5 us -> 57.7 us (0.986)
  starting transfers between devices: 32.3 us -> 34.9 us
  waiting for transfers between devices: 16 us -> 13.7 us
  Pallas kernels: 9.04 us -> 7.95 us
    ppermute x10, waiting for transfers between devices: 14.4 us -> 12.5 us  [cycle_end(): lax.ppermute(value, axis, pairs)]
    ppermute x1, starting transfers between devices: 1.91 us -> 3.67 us  [cycle_end(): u_odd = lax.ppermute(u_odd, 'gy', odd)]
    pallas_call x1, Pallas kernels: 2.75 us -> 2.13 us  [update(): pl.pallas_call(update_kernel, out_shape=(f32(*iterate.shape), f32(*iterat...]
    ppermute x1 -> x2, waiting for transfers between devices: 1.57 us -> 1.16 us  [the longest x1 1.16 us: cycle_end(): value = part + lax.ppermute(part, GZ, same)]
  transfers between devices with their start and end apart: 18 -> 19, of which waited for: 8 -> 8; matrix products, arithmetic and copies ran while one was open for 0% -> 0% of each run, Pallas kernels for 6% -> 5%
where the time goes in v3:
time: 57.7 us; the launch traced here: 57.5 us
  starting transfers between devices  34.9 us (60%)
  waiting for transfers between devices  13.7 us (24%)
  Pallas kernels  7.95 us (14%)
  between operations  0.91 us (2%)
    ppermute x10, starting transfers between devices, cycle_end(): lax.ppermute(value, axis, pairs)  16.2 us
    ppermute x10, waiting for transfers between devices, cycle_end(): lax.ppermute(value, axis, pairs)  12.5 us
    ppermute x1, starting transfers between devices, cycle_end(): k_cross = lax.ppermute(k_cross, GZ, cross)  4.56 us
    ppermute x1, starting transfers between devices, cycle_end(): k_odd = lax.ppermute(k_odd, 'gy', odd)  4.31 us
    ppermute x1, starting transfers between devices, cycle_end(): u_odd = lax.ppermute(u_odd, 'gy', odd)  3.67 us
    ppermute x1, starting transfers between devices, cycle_end(): u_even = lax.ppermute(u_even, 'gy', even)  3.51 us
    pallas_call x1, Pallas kernels, sketch(): pl.pallas_call(sketch_kernel, out_shape=(field, f32(nz, nx), f32(nz, nx),...  2.62 us
    pallas_call x1, Pallas kernels, update(): pl.pallas_call(update_kernel, out_shape=(f32(*iterate.shape), f32(*iterat...  2.13 us
  transfers between devices with their start and end apart: 19, of which 8 were waited for; matrix products, arithmetic and copies ran while one was open for 0% of the time, Pallas kernels for 5%

profile of v3, /device:TPU:40, one launch (start us, length us, event | category | flops | bytes accessed | tf_op | source)
XLA Modules:
  0.0 57.5 jit_solution(8130749244171454439)
XLA Ops:
  0.6 0.0 copy-start.5
  0.6 0.0 slice-start
  0.7 0.0 copy-start
  0.7 0.0 slice-start.1
  0.7 1.5 %edges.1 = (f32[72,1024]{1,0:T(8,128)S(1)}, f32[72,1024]{1,0:T(8,128)S(1)}, f32[8,1024]{1,0:T(8,128)S(1)}, f32[8,1024]{1,0:T(8,128)S(1)}) custom-call(f32[2,64,1024]{2,1,0:T(8,128)} %k_ref.1, s32[2,8,64]{2,1,0:T(8,128)} %bitcast.34, s32[2,8,64]{2,1,0:T(8,128)} %bitcast.36), custom_call_target="tpu_custom_call" | custom-call | flops 4294967296 | bytes 268435456 | tf_op jit(solution)/shard_map/edges/pallas_call | solution.py:82
  2.2 0.0 copy-start.1
  2.2 0.0 copy-start.2
  2.2 0.0 copy-start.3
  2.2 0.0 copy-start.4
  2.2 0.1 collective-permute-start
  2.3 4.6 %collective-permute-start.1 = (f32[72,1024]{1,0:T(8,128)S(1)}, f32[72,1024]{1,0:T(8,128)S(1)}, u32[]{:S(2)}, u32[]{:S(2)}) collective-permute-start(f32[72,1024]{1,0:T(8,128)S(1)} %get-tuple-element.23), channel_id=1, source_target_pairs={{4,8},{12,16},{20,24},{28,32},{36,40},{44,48},{52,56},{60,64},{68,... | collective-permute-start | bytes 884744 | tf_op jit(solution)/shard_map/ppermute | solution.py:410
  6.9 0.5 collective-permute-start.2
  7.5 4.3 %collective-permute-start.3 = (f32[8,1024]{1,0:T(8,128)S(1)}, f32[8,1024]{1,0:T(8,128)S(1)}, u32[]{:S(2)}, u32[]{:S(2)}) collective-permute-start(f32[8,1024]{1,0:T(8,128)S(1)} %get-tuple-element.25), channel_id=1, source_target_pairs={{1,2},{2,1},{0,0},{3,3},{5,6},{6,5},{4,4},{7,7},{9,10},{10,9},{8,8... | collective-permute-start | bytes 98312 | tf_op jit(solution)/shard_map/ppermute | solution.py:413
  11.8 0.0 copy-done.5
  11.8 0.0 slice-done
  11.8 0.0 copy-done
  11.8 0.0 slice-done.1
  11.8 2.1 %update.1 = (f32[2,512,128]{2,1,0:T(8,128)S(1)}, f32[512,128]{1,0:T(8,128)S(1)}, f32[512,128]{1,0:T(8,128)S(1)}) custom-call(f32[1,32]{1,0:T(1,128)S(1)} %bitcast.38, f32[2,512,128]{2,1,0:T(8,128)S(1)} %bitcast.32, bf16[32,2,512,128]{3,2,1,0:T(8,128)(2,1)S(1)} %bitcast.31), custom_call_target="tpu_custom_call" | custom-call | flops 16777216 | bytes 8388608 | tf_op jit(solution)/shard_map/update/pallas_call | solution.py:132
  13.9 0.0 collective-permute-done.2.even_ref
  14.0 0.0 collective-permute-done.3.odd_ref
  14.0 0.0 collective-permute-done.same_ref
  14.0 0.0 collective-permute-done.1.cross_ref
  14.0 0.0 copy-done.1
  14.0 0.0 copy-done.2
  14.0 0.0 copy-done.3
  14.0 0.0 copy-done.4
  14.0 2.6 %sketch.1 = (f32[2,64,1024]{2,1,0:T(8,128)}, f32[2,1024]{1,0:T(2,128)S(1)}, f32[2,1024]{1,0:T(2,128)S(1)}, f32[2,64,1024]{2,1,0:T(8,128)S(1)}, f32[2,64,1024]{2,...) custom-call(f32[2,64,1024]{2,1,0:T(8,128)S(1)} %bitcast.33, f32[2,64,1024]{2,1,0:T(8,128)S(1)} %copy-done.1, ...), custom_call_target="tpu_custom_call" | custom-call | flops 16777216 | bytes 16777216 | tf_op jit(solution)/shard_map/sketch/pallas_call | solution.py:307
  16.7 0.1 collective-permute-start.5
  16.8 1.2 %collective-permute-done.5 = f32[2,1024]{1,0:T(2,128)S(1)} collective-permute-done((f32[2,1024]{1,0:T(2,128)S(1)}, f32[2,1024]{1,0:T(2,128)S(1)}, u32[]{:S(2)}, u32[]{:S(2)}) %collective-permute-start.5) | collective-permute-done | bytes 8224 | tf_op jit(solution)/shard_map/ppermute | solution.py:419
  17.9 0.0 collective-permute-start.8
  17.9 3.1 %collective-permute-start.7 = (f32[2,1024]{1,0:T(2,128)S(1)}, f32[2,1024]{1,0:T(2,128)S(1)}, u32[]{:S(2)}, u32[]{:S(2)}) collective-permute-start(f32[2,1024]{1,0:T(2,128)S(1)} %add.24), channel_id=1, source_target_pairs={{0,2},{1,3},{2,0},{3,1},{4,6},{5,7},{6,4},{7,5},{8,10},{9,11},{10,... | collective-permute-start | bytes 24584 | tf_op jit(solution)/shard_map/ppermute | solution.py:426
  21.1 0.4 collective-permute-start.6
  21.4 0.0 collective-permute-start.4
  21.4 0.2 collective-permute-done.8
  21.6 1.6 %collective-permute-done.7 = f32[2,1024]{1,0:T(2,128)S(1)} collective-permute-done((f32[2,1024]{1,0:T(2,128)S(1)}, f32[2,1024]{1,0:T(2,128)S(1)}, u32[]{:S(2)}, u32[]{:S(2)}) %collective-permute-start.7) | collective-permute-done | bytes 8224 | tf_op jit(solution)/shard_map/ppermute | solution.py:426
  23.2 1.5 %collective-permute-done.6 = f32[2,1024]{1,0:T(2,128)S(1)} collective-permute-done((f32[2,1024]{1,0:T(2,128)S(1)}, f32[2,1024]{1,0:T(2,128)S(1)}, u32[]{:S(2)}, u32[]{:S(2)}) %collective-permute-start.6) | collective-permute-done | bytes 8224 | tf_op jit(solution)/shard_map/ppermute | solution.py:426
  24.7 1.9 %collective-permute-start.9 = (f32[64,1024]{1,0:T(8,128)S(1)}, f32[64,1024]{1,0:T(8,128)S(1)}, u32[]{:S(2)}, u32[]{:S(2)}) collective-permute-start(f32[64,1024]{1,0:T(8,128)S(1)} %bitcast.39), channel_id=1, source_target_pairs={{4,8},{12,16},{20,24},{28,32},{36,40},{44,48},{52,56},{60,64},{68,... | collective-permute-start | bytes 786440 | tf_op jit(solution)/shard_map/ppermute | solution.py:427
  26.7 0.3 collective-permute-start.14
  26.9 2.8 %collective-permute-start.13 = (f32[2,1024]{1,0:T(2,128)S(1)}, f32[2,1024]{1,0:T(2,128)S(1)}, u32[]{:S(2)}, u32[]{:S(2)}) collective-permute-start(f32[2,1024]{1,0:T(2,128)S(1)} %add_add_fusion.1), channel_id=1, source_target_pairs={{0,16},{8,24},{16,0},{24,8},{1,17},{9,25},{17,1},{25,9},{2,18},{10... | collective-permute-start | bytes 24584 | tf_op jit(solution)/shard_map/ppermute | solution.py:426
  29.8 1.7 %collective-permute-start.12 = (f32[2,1024]{1,0:T(2,128)S(1)}, f32[2,1024]{1,0:T(2,128)S(1)}, u32[]{:S(2)}, u32[]{:S(2)}) collective-permute-start(f32[2,1024]{1,0:T(2,128)S(1)} %add_add_fusion.1), channel_id=1, source_target_pairs={{0,24},{8,16},{16,8},{24,0},{1,25},{9,17},{17,9},{25,1},{2,26},{10... | collective-permute-start | bytes 24584 | tf_op jit(solution)/shard_map/ppermute | solution.py:426
  31.4 0.0 collective-permute-done.14
  31.4 0.8 %collective-permute-done.13 = f32[2,1024]{1,0:T(2,128)S(1)} collective-permute-done((f32[2,1024]{1,0:T(2,128)S(1)}, f32[2,1024]{1,0:T(2,128)S(1)}, u32[]{:S(2)}, u32[]{:S(2)}) %collective-permute-start.13) | collective-permute-done | bytes 8224 | tf_op jit(solution)/shard_map/ppermute | solution.py:426
  32.3 2.5 %collective-permute-done.12 = f32[2,1024]{1,0:T(2,128)S(1)} collective-permute-done((f32[2,1024]{1,0:T(2,128)S(1)}, f32[2,1024]{1,0:T(2,128)S(1)}, u32[]{:S(2)}, u32[]{:S(2)}) %collective-permute-start.12) | collective-permute-done | bytes 8224 | tf_op jit(solution)/shard_map/ppermute | solution.py:426
  34.8 0.1 collective-permute-start.15
  34.9 3.6 %collective-permute-done.15 = f32[2,1024]{1,0:T(2,128)S(1)} collective-permute-done((f32[2,1024]{1,0:T(2,128)S(1)}, f32[2,1024]{1,0:T(2,128)S(1)}, u32[]{:S(2)}, u32[]{:S(2)}) %collective-permute-start.15) | collective-permute-done | bytes 8224 | tf_op jit(solution)/shard_map/ppermute | solution.py:426
  38.5 2.9 %collective-permute-start.18 = (f32[2,1024]{1,0:T(2,128)S(1)}, f32[2,1024]{1,0:T(2,128)S(1)}, u32[]{:S(2)}, u32[]{:S(2)}) collective-permute-start(f32[2,1024]{1,0:T(2,128)S(1)} %add.31.refs_0_), channel_id=1, source_target_pairs={{32,64},{96,128},{160,192},{224,0},{64,32},{128,96},{192,160},{0,2... | collective-permute-start | bytes 24584 | tf_op jit(solution)/shard_map/ppermute | solution.py:426
  41.4 4.2 %collective-permute-start.17 = (f32[2,1024]{1,0:T(2,128)S(1)}, f32[2,1024]{1,0:T(2,128)S(1)}, u32[]{:S(2)}, u32[]{:S(2)}) collective-permute-start(f32[2,1024]{1,0:T(2,128)S(1)} %add.31.refs_0_), channel_id=1, source_target_pairs={{0,192},{64,0},{128,64},{192,128},{32,96},{96,160},{160,224},{224,... | collective-permute-start | bytes 24584 | tf_op jit(solution)/shard_map/ppermute | solution.py:426
  45.6 3.5 %collective-permute-start.10 = (f32[2,1024]{1,0:T(2,128)S(1)}, f32[2,1024]{1,0:T(2,128)S(1)}, u32[]{:S(2)}, u32[]{:S(2)}) collective-permute-start(f32[2,1024]{1,0:T(2,128)S(1)} %get-tuple-element.36), channel_id=1, source_target_pairs={{0,1},{2,3},{1,0},{3,2},{4,5},{6,7},{5,4},{7,6},{8,9},{10,11},{9,8... | collective-permute-start | bytes 24584 | tf_op jit(solution)/shard_map/ppermute | solution.py:429
  49.1 0.0 collective-permute-done.18.refs_3_
  49.1 0.8 %collective-permute-start.16 = (f32[2,1024]{1,0:T(2,128)S(1)}, f32[2,1024]{1,0:T(2,128)S(1)}, u32[]{:S(2)}, u32[]{:S(2)}) collective-permute-start(f32[2,1024]{1,0:T(2,128)S(1)} %add.31.refs_0_), channel_id=1, source_target_pairs={{0,160},{32,128},{64,224},{96,192},{160,0},{128,32},{224,64},{192,... | collective-permute-start | bytes 24584 | tf_op jit(solution)/shard_map/ppermute | solution.py:426
  49.9 0.0 collective-permute-done.17.refs_2_
  49.9 3.7 %collective-permute-start.11 = (f32[2,1024]{1,0:T(2,128)S(1)}, f32[2,1024]{1,0:T(2,128)S(1)}, u32[]{:S(2)}, u32[]{:S(2)}) collective-permute-start(f32[2,1024]{1,0:T(2,128)S(1)} %get-tuple-element.37), channel_id=1, source_target_pairs={{1,2},{2,1},{0,0},{3,3},{5,6},{6,5},{4,4},{7,7},{9,10},{10,9},{8,8... | collective-permute-start | bytes 24584 | tf_op jit(solution)/shard_map/ppermute | solution.py:430
  53.6 2.2 %collective-permute-done.16.refs_1_ = f32[2,1024]{1,0:T(2,128)S(1)} collective-permute-done((f32[2,1024]{1,0:T(2,128)S(1)}, f32[2,1024]{1,0:T(2,128)S(1)}, u32[]{:S(2)}, u32[]{:S(2)}) %collective-permute-start.16) | collective-permute-done | bytes 8224 | tf_op jit(solution)/shard_map/ppermute | solution.py:426
  55.8 0.8 %scaled.1 = f32[16,128]{1,0:T(8,128)} custom-call(f32[2,1024]{1,0:T(2,128)S(1)} %add.31.refs_0_, f32[2,1024]{1,0:T(2,128)S(1)} %collective-permute-done.16.refs_1_, f32[2,1024]{1,0:T(2,128)S(1)} %collective-permute-done.17.refs_2_, f32[2,1024]{1,0:T(2,128)S(1)} %collective-permute-done.18.refs_3_), custom_call_target="tpu_custom_call" | custom-call | tf_op jit(solution)/shard_map/scaled/pallas_call | solution.py:368
  56.5 0.0 collective-permute-done.10.ue_ref
  56.5 0.0 collective-permute-done.11.uo_ref
  56.5 0.0 collective-permute-done.4.us_ref
  56.5 0.0 collective-permute-done.9.uc_ref
  56.5 0.9 %halo.1 = f32[2,64,1024]{2,1,0:T(8,128)} custom-call(f32[2,64,1024]{2,1,0:T(8,128)S(1)} %get-tuple-element.27.base_ref, f32[2,64,1024]{2,1,0:T(8,128)S(1)} %get-tuple-element.28.wz_ref, f32[4,1024]{1,0:T(4,128)S(1)} %get-tuple-element.29.wy_ref, f32[64,1024]{1,0:T(8,128)S(1)} %collective-permute-done.4.us_ref, f32[64,1024]{1,0:T(8,128)S(1)} %collective-permute-done.9.uc_ref, ...), custom_call_target="tpu_custom_call" | custom-call | flops 1048576 | bytes 2097152 | tf_op jit(solution)/shard_map/halo/pallas_call | solution.py:345
  (5 shorter events, 0.0 us)
Async XLA Ops:
  0.6 11.1 %copy-start.5 = (f32[32]{0:T(128)S(1)}, f32[32]{0:T(128)}, u32[]{:S(2)}) copy-start(f32[32]{0:T(128)} %param.9) | copy-start | bytes 388
  0.6 11.1 %slice-start = ((s8[8388608]{0:T(1024)(128)(4,1)}), s8[4194304]{0:T(1024)(128)(4,1)S(1)}, s32[]{:S(2)}) async-start(s8[8388608]{0:T(1024)(128)(4,1)} %bitcast.29), calls=%async_computation | async-start | bytes 8388608
  0.7 11.1 %copy-start = (f32[2,64,1024]{2,1,0:T(8,128)S(1)}, f32[2,64,1024]{2,1,0:T(8,128)}, u32[]{:S(2)}) copy-start(f32[2,64,1024]{2,1,0:T(8,128)} %param.7) | copy-start | bytes 1572868
  0.7 11.1 %slice-start.1 = ((s8[8388608]{0:T(1024)(128)(4,1)}), s8[4194304]{0:T(1024)(128)(4,1)S(1)}, s32[]{:S(2)}) async-start(s8[8388608]{0:T(1024)(128)(4,1)} %bitcast.29), calls=%async_computation.1 | async-start | bytes 8388608
  2.2 11.8 %copy-start.1 = (f32[2,64,1024]{2,1,0:T(8,128)S(1)}, f32[2,64,1024]{2,1,0:T(8,128)}, u32[]{:S(2)}) copy-start(f32[2,64,1024]{2,1,0:T(8,128)} %k_ref.1) | copy-start | bytes 1572868
  2.2 11.8 %copy-start.2 = (f32[2,64,1024]{2,1,0:T(8,128)S(1)}, f32[2,64,1024]{2,1,0:T(8,128)}, u32[]{:S(2)}) copy-start(f32[2,64,1024]{2,1,0:T(8,128)} %rhs_ref.1) | copy-start | bytes 1572868
  2.2 11.8 %copy-start.3 = (s32[2,64,8]{1,2,0:T(8,128)S(1)}, s32[2,64,8]{1,2,0:T(8,128)}, u32[]{:S(2)}) copy-start(s32[2,64,8]{1,2,0:T(8,128)} %param.12) | copy-start | bytes 12292
  2.2 11.8 %copy-start.4 = (s32[2,64,8]{1,2,0:T(8,128)S(1)}, s32[2,64,8]{1,2,0:T(8,128)}, u32[]{:S(2)}) copy-start(s32[2,64,8]{1,2,0:T(8,128)} %param.13) | copy-start | bytes 12292
  2.2 11.7 %collective-permute-start = (f32[72,1024]{1,0:T(8,128)S(1)}, f32[72,1024]{1,0:T(8,128)S(1)}, u32[]{:S(2)}, u32[]{:S(2)}) collective-permute-start(f32[72,1024]{1,0:T(8,128)S(1)} %get-tuple-element.22), channel_id=1, source_target_pairs={{0,4},{8,12},{16,20},{24,28},{32,36},{40,44},{48,52},{56,60},{64,6... | collective-permute-start | bytes 884744 | tf_op jit(solution)/shard_map/ppermute | solution.py:411
  2.3 11.6 %collective-permute-start.1 = (f32[72,1024]{1,0:T(8,128)S(1)}, f32[72,1024]{1,0:T(8,128)S(1)}, u32[]{:S(2)}, u32[]{:S(2)}) collective-permute-start(f32[72,1024]{1,0:T(8,128)S(1)} %get-tuple-element.23), channel_id=1, source_target_pairs={{4,8},{12,16},{20,24},{28,32},{36,40},{44,48},{52,56},{60,64},{68,... | collective-permute-start | bytes 884744 | tf_op jit(solution)/shard_map/ppermute | solution.py:410
  6.9 7.0 %collective-permute-start.2 = (f32[8,1024]{1,0:T(8,128)S(1)}, f32[8,1024]{1,0:T(8,128)S(1)}, u32[]{:S(2)}, u32[]{:S(2)}) collective-permute-start(f32[8,1024]{1,0:T(8,128)S(1)} %get-tuple-element.24), channel_id=1, source_target_pairs={{0,1},{2,3},{1,0},{3,2},{4,5},{6,7},{5,4},{7,6},{8,9},{10,11},{9,8... | collective-permute-start | bytes 98312 | tf_op jit(solution)/shard_map/ppermute | solution.py:412
  7.5 6.5 %collective-permute-start.3 = (f32[8,1024]{1,0:T(8,128)S(1)}, f32[8,1024]{1,0:T(8,128)S(1)}, u32[]{:S(2)}, u32[]{:S(2)}) collective-permute-start(f32[8,1024]{1,0:T(8,128)S(1)} %get-tuple-element.25), channel_id=1, source_target_pairs={{1,2},{2,1},{0,0},{3,3},{5,6},{6,5},{4,4},{7,7},{9,10},{10,9},{8,8... | collective-permute-start | bytes 98312 | tf_op jit(solution)/shard_map/ppermute | solution.py:413
  16.7 1.3 %collective-permute-start.5 = (f32[2,1024]{1,0:T(2,128)S(1)}, f32[2,1024]{1,0:T(2,128)S(1)}, u32[]{:S(2)}, u32[]{:S(2)}) collective-permute-start(f32[2,1024]{1,0:T(2,128)S(1)} %get-tuple-element.34), channel_id=1, source_target_pairs={{0,4},{8,12},{16,20},{24,28},{32,36},{40,44},{48,52},{56,60},{64,6... | collective-permute-start | bytes 24584 | tf_op jit(solution)/shard_map/ppermute | solution.py:419
  17.9 3.7 %collective-permute-start.8 = (f32[2,1024]{1,0:T(2,128)S(1)}, f32[2,1024]{1,0:T(2,128)S(1)}, u32[]{:S(2)}, u32[]{:S(2)}) collective-permute-start(f32[2,1024]{1,0:T(2,128)S(1)} %add.24), channel_id=1, source_target_pairs={{0,1},{1,0},{2,3},{3,2},{4,5},{5,4},{6,7},{7,6},{8,9},{9,8},{10,11... | collective-permute-start | bytes 24584 | tf_op jit(solution)/shard_map/ppermute | solution.py:426
  17.9 5.2 %collective-permute-start.7 = (f32[2,1024]{1,0:T(2,128)S(1)}, f32[2,1024]{1,0:T(2,128)S(1)}, u32[]{:S(2)}, u32[]{:S(2)}) collective-permute-start(f32[2,1024]{1,0:T(2,128)S(1)} %add.24), channel_id=1, source_target_pairs={{0,2},{1,3},{2,0},{3,1},{4,6},{5,7},{6,4},{7,5},{8,10},{9,11},{10,... | collective-permute-start | bytes 24584 | tf_op jit(solution)/shard_map/ppermute | solution.py:426
  21.1 3.7 %collective-permute-start.6 = (f32[2,1024]{1,0:T(2,128)S(1)}, f32[2,1024]{1,0:T(2,128)S(1)}, u32[]{:S(2)}, u32[]{:S(2)}) collective-permute-start(f32[2,1024]{1,0:T(2,128)S(1)} %add.24), channel_id=1, source_target_pairs={{0,3},{1,2},{2,1},{3,0},{4,7},{5,6},{6,5},{7,4},{8,11},{9,10},{10,... | collective-permute-start | bytes 24584 | tf_op jit(solution)/shard_map/ppermute | solution.py:426
  21.4 35.1 %collective-permute-start.4 = (f32[64,1024]{1,0:T(8,128)S(1)}, f32[64,1024]{1,0:T(8,128)S(1)}, u32[]{:S(2)}, u32[]{:S(2)}) collective-permute-start(f32[64,1024]{1,0:T(8,128)S(1)} %bitcast.40), channel_id=1, source_target_pairs={{0,4},{8,12},{16,20},{24,28},{32,36},{40,44},{48,52},{56,60},{64,6... | collective-permute-start | bytes 786440 | tf_op jit(solution)/shard_map/ppermute | solution.py:428
  24.7 31.8 %collective-permute-start.9 = (f32[64,1024]{1,0:T(8,128)S(1)}, f32[64,1024]{1,0:T(8,128)S(1)}, u32[]{:S(2)}, u32[]{:S(2)}) collective-permute-start(f32[64,1024]{1,0:T(8,128)S(1)} %bitcast.39), channel_id=1, source_target_pairs={{4,8},{12,16},{20,24},{28,32},{36,40},{44,48},{52,56},{60,64},{68,... | collective-permute-start | bytes 786440 | tf_op jit(solution)/shard_map/ppermute | solution.py:427
  26.7 4.8 %collective-permute-start.14 = (f32[2,1024]{1,0:T(2,128)S(1)}, f32[2,1024]{1,0:T(2,128)S(1)}, u32[]{:S(2)}, u32[]{:S(2)}) collective-permute-start(f32[2,1024]{1,0:T(2,128)S(1)} %add_add_fusion.1), channel_id=1, source_target_pairs={{0,8},{8,0},{16,24},{24,16},{1,9},{9,1},{17,25},{25,17},{2,10},{10... | collective-permute-start | bytes 24584 | tf_op jit(solution)/shard_map/ppermute | solution.py:426
  26.9 5.3 %collective-permute-start.13 = (f32[2,1024]{1,0:T(2,128)S(1)}, f32[2,1024]{1,0:T(2,128)S(1)}, u32[]{:S(2)}, u32[]{:S(2)}) collective-permute-start(f32[2,1024]{1,0:T(2,128)S(1)} %add_add_fusion.1), channel_id=1, source_target_pairs={{0,16},{8,24},{16,0},{24,8},{1,17},{9,25},{17,1},{25,9},{2,18},{10... | collective-permute-start | bytes 24584 | tf_op jit(solution)/shard_map/ppermute | solution.py:426
  29.8 5.0 %collective-permute-start.12 = (f32[2,1024]{1,0:T(2,128)S(1)}, f32[2,1024]{1,0:T(2,128)S(1)}, u32[]{:S(2)}, u32[]{:S(2)}) collective-permute-start(f32[2,1024]{1,0:T(2,128)S(1)} %add_add_fusion.1), channel_id=1, source_target_pairs={{0,24},{8,16},{16,8},{24,0},{1,25},{9,17},{17,9},{25,1},{2,26},{10... | collective-permute-start | bytes 24584 | tf_op jit(solution)/shard_map/ppermute | solution.py:426
  34.8 3.7 %collective-permute-start.15 = (f32[2,1024]{1,0:T(2,128)S(1)}, f32[2,1024]{1,0:T(2,128)S(1)}, u32[]{:S(2)}, u32[]{:S(2)}) collective-permute-start(f32[2,1024]{1,0:T(2,128)S(1)} %add_add_fusion), channel_id=1, source_target_pairs={{0,32},{64,96},{128,160},{192,224},{32,0},{96,64},{160,128},{224,1... | collective-permute-start | bytes 24584 | tf_op jit(solution)/shard_map/ppermute | solution.py:426
  38.5 10.5 %collective-permute-start.18 = (f32[2,1024]{1,0:T(2,128)S(1)}, f32[2,1024]{1,0:T(2,128)S(1)}, u32[]{:S(2)}, u32[]{:S(2)}) collective-permute-start(f32[2,1024]{1,0:T(2,128)S(1)} %add.31.refs_0_), channel_id=1, source_target_pairs={{32,64},{96,128},{160,192},{224,0},{64,32},{128,96},{192,160},{0,2... | collective-permute-start | bytes 24584 | tf_op jit(solution)/shard_map/ppermute | solution.py:426
  41.4 8.5 %collective-permute-start.17 = (f32[2,1024]{1,0:T(2,128)S(1)}, f32[2,1024]{1,0:T(2,128)S(1)}, u32[]{:S(2)}, u32[]{:S(2)}) collective-permute-start(f32[2,1024]{1,0:T(2,128)S(1)} %add.31.refs_0_), channel_id=1, source_target_pairs={{0,192},{64,0},{128,64},{192,128},{32,96},{96,160},{160,224},{224,... | collective-permute-start | bytes 24584 | tf_op jit(solution)/shard_map/ppermute | solution.py:426
  45.6 10.9 %collective-permute-start.10 = (f32[2,1024]{1,0:T(2,128)S(1)}, f32[2,1024]{1,0:T(2,128)S(1)}, u32[]{:S(2)}, u32[]{:S(2)}) collective-permute-start(f32[2,1024]{1,0:T(2,128)S(1)} %get-tuple-element.36), channel_id=1, source_target_pairs={{0,1},{2,3},{1,0},{3,2},{4,5},{6,7},{5,4},{7,6},{8,9},{10,11},{9,8... | collective-permute-start | bytes 24584 | tf_op jit(solution)/shard_map/ppermute | solution.py:429
  49.1 6.7 %collective-permute-start.16 = (f32[2,1024]{1,0:T(2,128)S(1)}, f32[2,1024]{1,0:T(2,128)S(1)}, u32[]{:S(2)}, u32[]{:S(2)}) collective-permute-start(f32[2,1024]{1,0:T(2,128)S(1)} %add.31.refs_0_), channel_id=1, source_target_pairs={{0,160},{32,128},{64,224},{96,192},{160,0},{128,32},{224,64},{192,... | collective-permute-start | bytes 24584 | tf_op jit(solution)/shard_map/ppermute | solution.py:426
  49.9 6.6 %collective-permute-start.11 = (f32[2,1024]{1,0:T(2,128)S(1)}, f32[2,1024]{1,0:T(2,128)S(1)}, u32[]{:S(2)}, u32[]{:S(2)}) collective-permute-start(f32[2,1024]{1,0:T(2,128)S(1)} %get-tuple-element.37), channel_id=1, source_target_pairs={{1,2},{2,1},{0,0},{3,3},{5,6},{6,5},{4,4},{7,7},{9,10},{10,9},{8,8... | collective-permute-start | bytes 24584 | tf_op jit(solution)/shard_map/ppermute | solution.py:430

commit v4 on v3

--- a/solution.py
+++ b/solution.py
@@ -38,23 +38,30 @@
     return [jnp.where(edge, 0.0, 1.0) for edge in outer]
 
 
-def edge_kernel(k_hbm, off_hbm, flip_hbm, same_ref, cross_ref, even_ref, odd_ref, k_ref, off_ref, flip_ref, sems):
-    copies = [
-        pltpu.make_async_copy(source, target, sems.at[i])
-        for i, (source, target) in enumerate(((k_hbm, k_ref), (off_hbm, off_ref), (flip_hbm, flip_ref)))
-    ]
+def edge_kernel(
+    k_hbm, off_hbm, flip_hbm, same_ref, cross_ref, even_ref, odd_ref, low_ref, high_ref, off_ref, flip_ref, sems
+):
+    nz, ny, nx = k_hbm.shape
+    core = lax.axis_index("core")
+    moves = (
+        (off_hbm, off_ref),
+        (flip_hbm, flip_ref),
+        (k_hbm.at[:, pl.ds(0, 8), :], low_ref),
+        (k_hbm.at[:, pl.ds(ny - 8, 8), :], high_ref),
+        (k_hbm.at[core], cross_ref.at[pl.ds(0, ny), :]),
+        (k_hbm.at[1 - core], same_ref.at[pl.ds(0, ny), :]),
+    )
+    copies = [pltpu.make_async_copy(source, target, sems.at[i]) for i, (source, target) in enumerate(moves)]
     for copy in copies:
         copy.start()
-    for copy in copies:
+    for copy in copies[:4]:
         copy.wait()
-    nz, ny, nx = k_ref.shape
     blocks = nx // BLK
     core0, even = parities()
 
     def both(low, high):
         return jnp.where(core0, high, low), jnp.where(core0, low, high)
 
-    same_ref[:ny], cross_ref[:ny] = both(k_ref[0], k_ref[1])
     offs = [off_ref[z].astype(jnp.float32) for z in range(nz)]
     signs = [(2 * flip_ref[z] - 1).astype(jnp.float32) for z in range(nz)]
     same_ref[ny:, :ny], cross_ref[ny:, :ny] = both(offs[0], offs[1])
@@ -68,23 +75,27 @@
                 high = jnp.broadcast_to(table[ny - 1 :, q : q + 1], (1, BLK))
                 even_ref[at : at + 1, lanes] = jnp.where(even, high, low)
                 odd_ref[at : at + 1, lanes] = jnp.where(even, low, high)
-        low, high = k_ref[z, :1, :], k_ref[z, ny - 1 :, :]
+        low, high = low_ref[z, :1, :], high_ref[z, 7:, :]
         even_ref[z : z + 1, :] = jnp.where(even, high, low)
         odd_ref[z : z + 1, :] = jnp.where(even, low, high)
     rest = slice(3 * nz, 8)
     even_ref[rest, :] = jnp.zeros((8 - 3 * nz, nx), jnp.float32)
     odd_ref[rest, :] = jnp.zeros((8 - 3 * nz, nx), jnp.float32)
+    for copy in copies[4:]:
+        copy.wait()
 
 
 def edges(kappa, offsets, flips):
-    _, ny, nx = kappa.shape
+    nz, ny, nx = kappa.shape
     plane, line = f32(ny + 8, nx), f32(8, nx)
     return pl.pallas_call(
         edge_kernel,
         out_shape=(plane, plane, line, line),
         in_specs=[HBM] * 3,
         out_specs=(VMEM,) * 4,
-        scratch_shapes=[pltpu.VMEM(v.shape, v.dtype) for v in (kappa, offsets, flips)] + [pltpu.SemaphoreType.DMA((3,))],
+        scratch_shapes=[pltpu.VMEM((nz, 8, nx), jnp.float32)] * 2
+        + [pltpu.VMEM(v.shape, v.dtype) for v in (offsets, flips)]
+        + [pltpu.SemaphoreType.DMA((6,))],
         compiler_params=pltpu.CompilerParams(vmem_limit_bytes=8 << 20),
         cost_estimate=pl.CostEstimate(flops=1 << 32, bytes_accessed=1 << 28, transcendentals=0),
         name="edges",

time: 57.7 us -> 57.5 us (level)
  no operation moved by 1% of the time
where the time goes in v4:
time: 57.5 us; the launch traced here: 57.3 us
  starting transfers between devices  34.9 us (61%)
  waiting for transfers between devices  13.7 us (24%)
  Pallas kernels  7.82 us (14%)
  between operations  0.91 us (2%)
    ppermute x10, starting transfers between devices, cycle_end(): lax.ppermute(value, axis, pairs)  16.2 us
    ppermute x10, waiting for transfers between devices, cycle_end(): lax.ppermute(value, axis, pairs)  12.5 us
    ppermute x1, starting transfers between devices, cycle_end(): k_cross = lax.ppermute(k_cross, GZ, cross)  4.56 us
    ppermute x1, starting transfers between devices, cycle_end(): k_odd = lax.ppermute(k_odd, 'gy', odd)  4.31 us
    ppermute x1, starting transfers between devices, cycle_end(): u_odd = lax.ppermute(u_odd, 'gy', odd)  3.67 us
    ppermute x1, starting transfers between devices, cycle_end(): u_even = lax.ppermute(u_even, 'gy', even)  3.51 us
    pallas_call x1, Pallas kernels, sketch(): pl.pallas_call(sketch_kernel, out_shape=(field, f32(nz, nx), f32(nz, nx),...  2.62 us
    pallas_call x1, Pallas kernels, update(): pl.pallas_call(update_kernel, out_shape=(f32(*iterate.shape), f32(*iterat...  2.13 us
  transfers between devices with their start and end apart: 19, of which 8 were waited for; matrix products, arithmetic and copies ran while one was open for 0% of the time, Pallas kernels for 5%

profile of v4, /device:TPU:40, one launch (start us, length us, event | category | flops | bytes accessed | tf_op | source)
XLA Modules:
  0.0 57.3 jit_solution(10202670470955264329)
XLA Ops:
  0.6 0.0 copy-start.5
  0.6 0.0 slice-start
  0.7 0.0 copy-start
  0.7 0.0 slice-start.1
  0.7 1.4 %edges.1 = (f32[72,1024]{1,0:T(8,128)S(1)}, f32[72,1024]{1,0:T(8,128)S(1)}, f32[8,1024]{1,0:T(8,128)S(1)}, f32[8,1024]{1,0:T(8,128)S(1)}) custom-call(f32[2,64,1024]{2,1,0:T(8,128)} %k_ref.1, s32[2,8,64]{2,1,0:T(8,128)} %bitcast.34, s32[2,8,64]{2,1,0:T(8,128)} %bitcast.36), custom_call_target="tpu_custom_call" | custom-call | flops 4294967296 | bytes 268435456 | tf_op jit(solution)/shard_map/edges/pallas_call | solution.py:91
  2.1 0.0 copy-start.1
  2.1 0.0 copy-start.2
  2.1 0.0 copy-start.3
  2.1 0.0 copy-start.4
  2.1 0.1 collective-permute-start
  2.2 4.6 %collective-permute-start.1 = (f32[72,1024]{1,0:T(8,128)S(1)}, f32[72,1024]{1,0:T(8,128)S(1)}, u32[]{:S(2)}, u32[]{:S(2)}) collective-permute-start(f32[72,1024]{1,0:T(8,128)S(1)} %get-tuple-element.23), channel_id=1, source_target_pairs={{4,8},{12,16},{20,24},{28,32},{36,40},{44,48},{52,56},{60,64},{68,... | collective-permute-start | bytes 884744 | tf_op jit(solution)/shard_map/ppermute | solution.py:421
  6.8 0.5 collective-permute-start.2
  7.3 4.3 %collective-permute-start.3 = (f32[8,1024]{1,0:T(8,128)S(1)}, f32[8,1024]{1,0:T(8,128)S(1)}, u32[]{:S(2)}, u32[]{:S(2)}) collective-permute-start(f32[8,1024]{1,0:T(8,128)S(1)} %get-tuple-element.25), channel_id=1, source_target_pairs={{1,2},{2,1},{0,0},{3,3},{5,6},{6,5},{4,4},{7,7},{9,10},{10,9},{8,8... | collective-permute-start | bytes 98312 | tf_op jit(solution)/shard_map/ppermute | solution.py:424
  11.6 0.0 copy-done.5
  11.6 0.0 slice-done
  11.7 0.0 copy-done
  11.7 0.0 slice-done.1
  11.7 2.1 %update.1 = (f32[2,512,128]{2,1,0:T(8,128)S(1)}, f32[512,128]{1,0:T(8,128)S(1)}, f32[512,128]{1,0:T(8,128)S(1)}) custom-call(f32[1,32]{1,0:T(1,128)S(1)} %bitcast.38, f32[2,512,128]{2,1,0:T(8,128)S(1)} %bitcast.32, bf16[32,2,512,128]{3,2,1,0:T(8,128)(2,1)S(1)} %bitcast.31), custom_call_target="tpu_custom_call" | custom-call | flops 16777216 | bytes 8388608 | tf_op jit(solution)/shard_map/update/pallas_call | solution.py:143
  13.8 0.0 collective-permute-done.2.even_ref
  13.8 0.0 collective-permute-done.3.odd_ref
  13.8 0.0 collective-permute-done.same_ref
  13.8 0.0 collective-permute-done.1.cross_ref
  13.9 0.0 copy-done.1
  13.9 0.0 copy-done.2
  13.9 0.0 copy-done.3
  13.9 0.0 copy-done.4
  13.9 2.6 %sketch.1 = (f32[2,64,1024]{2,1,0:T(8,128)}, f32[2,1024]{1,0:T(2,128)S(1)}, f32[2,1024]{1,0:T(2,128)S(1)}, f32[2,64,1024]{2,1,0:T(8,128)S(1)}, f32[2,64,1024]{2,...) custom-call(f32[2,64,1024]{2,1,0:T(8,128)S(1)} %bitcast.33, f32[2,64,1024]{2,1,0:T(8,128)S(1)} %copy-done.1, ...), custom_call_target="tpu_custom_call" | custom-call | flops 16777216 | bytes 16777216 | tf_op jit(solution)/shard_map/sketch/pallas_call | solution.py:318
  16.5 0.1 collective-permute-start.5
  16.6 1.2 %collective-permute-done.5 = f32[2,1024]{1,0:T(2,128)S(1)} collective-permute-done((f32[2,1024]{1,0:T(2,128)S(1)}, f32[2,1024]{1,0:T(2,128)S(1)}, u32[]{:S(2)}, u32[]{:S(2)}) %collective-permute-start.5) | collective-permute-done | bytes 8224 | tf_op jit(solution)/shard_map/ppermute | solution.py:430
  17.8 0.0 collective-permute-start.8
  17.8 3.1 %collective-permute-start.7 = (f32[2,1024]{1,0:T(2,128)S(1)}, f32[2,1024]{1,0:T(2,128)S(1)}, u32[]{:S(2)}, u32[]{:S(2)}) collective-permute-start(f32[2,1024]{1,0:T(2,128)S(1)} %add.24), channel_id=1, source_target_pairs={{0,2},{1,3},{2,0},{3,1},{4,6},{5,7},{6,4},{7,5},{8,10},{9,11},{10,... | collective-permute-start | bytes 24584 | tf_op jit(solution)/shard_map/ppermute | solution.py:437
  20.9 0.4 collective-permute-start.6
  21.3 0.0 collective-permute-start.4
  21.3 0.2 collective-permute-done.8
  21.4 1.6 %collective-permute-done.7 = f32[2,1024]{1,0:T(2,128)S(1)} collective-permute-done((f32[2,1024]{1,0:T(2,128)S(1)}, f32[2,1024]{1,0:T(2,128)S(1)}, u32[]{:S(2)}, u32[]{:S(2)}) %collective-permute-start.7) | collective-permute-done | bytes 8224 | tf_op jit(solution)/shard_map/ppermute | solution.py:437
  23.0 1.5 %collective-permute-done.6 = f32[2,1024]{1,0:T(2,128)S(1)} collective-permute-done((f32[2,1024]{1,0:T(2,128)S(1)}, f32[2,1024]{1,0:T(2,128)S(1)}, u32[]{:S(2)}, u32[]{:S(2)}) %collective-permute-start.6) | collective-permute-done | bytes 8224 | tf_op jit(solution)/shard_map/ppermute | solution.py:437
  24.6 1.9 %collective-permute-start.9 = (f32[64,1024]{1,0:T(8,128)S(1)}, f32[64,1024]{1,0:T(8,128)S(1)}, u32[]{:S(2)}, u32[]{:S(2)}) collective-permute-start(f32[64,1024]{1,0:T(8,128)S(1)} %bitcast.39), channel_id=1, source_target_pairs={{4,8},{12,16},{20,24},{28,32},{36,40},{44,48},{52,56},{60,64},{68,... | collective-permute-start | bytes 786440 | tf_op jit(solution)/shard_map/ppermute | solution.py:438
  26.5 0.3 collective-permute-start.14
  26.8 2.8 %collective-permute-start.13 = (f32[2,1024]{1,0:T(2,128)S(1)}, f32[2,1024]{1,0:T(2,128)S(1)}, u32[]{:S(2)}, u32[]{:S(2)}) collective-permute-start(f32[2,1024]{1,0:T(2,128)S(1)} %add_add_fusion.1), channel_id=1, source_target_pairs={{0,16},{8,24},{16,0},{24,8},{1,17},{9,25},{17,1},{25,9},{2,18},{10... | collective-permute-start | bytes 24584 | tf_op jit(solution)/shard_map/ppermute | solution.py:437
  29.6 1.7 %collective-permute-start.12 = (f32[2,1024]{1,0:T(2,128)S(1)}, f32[2,1024]{1,0:T(2,128)S(1)}, u32[]{:S(2)}, u32[]{:S(2)}) collective-permute-start(f32[2,1024]{1,0:T(2,128)S(1)} %add_add_fusion.1), channel_id=1, source_target_pairs={{0,24},{8,16},{16,8},{24,0},{1,25},{9,17},{17,9},{25,1},{2,26},{10... | collective-permute-start | bytes 24584 | tf_op jit(solution)/shard_map/ppermute | solution.py:437
  31.3 0.0 collective-permute-done.14
  31.3 0.8 %collective-permute-done.13 = f32[2,1024]{1,0:T(2,128)S(1)} collective-permute-done((f32[2,1024]{1,0:T(2,128)S(1)}, f32[2,1024]{1,0:T(2,128)S(1)}, u32[]{:S(2)}, u32[]{:S(2)}) %collective-permute-start.13) | collective-permute-done | bytes 8224 | tf_op jit(solution)/shard_map/ppermute | solution.py:437
  32.1 2.5 %collective-permute-done.12 = f32[2,1024]{1,0:T(2,128)S(1)} collective-permute-done((f32[2,1024]{1,0:T(2,128)S(1)}, f32[2,1024]{1,0:T(2,128)S(1)}, u32[]{:S(2)}, u32[]{:S(2)}) %collective-permute-start.12) | collective-permute-done | bytes 8224 | tf_op jit(solution)/shard_map/ppermute | solution.py:437
  34.7 0.1 collective-permute-start.15
  34.8 3.6 %collective-permute-done.15 = f32[2,1024]{1,0:T(2,128)S(1)} collective-permute-done((f32[2,1024]{1,0:T(2,128)S(1)}, f32[2,1024]{1,0:T(2,128)S(1)}, u32[]{:S(2)}, u32[]{:S(2)}) %collective-permute-start.15) | collective-permute-done | bytes 8224 | tf_op jit(solution)/shard_map/ppermute | solution.py:437
  38.4 2.9 %collective-permute-start.18 = (f32[2,1024]{1,0:T(2,128)S(1)}, f32[2,1024]{1,0:T(2,128)S(1)}, u32[]{:S(2)}, u32[]{:S(2)}) collective-permute-start(f32[2,1024]{1,0:T(2,128)S(1)} %add.31.refs_0_), channel_id=1, source_target_pairs={{32,64},{96,128},{160,192},{224,0},{64,32},{128,96},{192,160},{0,2... | collective-permute-start | bytes 24584 | tf_op jit(solution)/shard_map/ppermute | solution.py:437
  41.3 4.2 %collective-permute-start.17 = (f32[2,1024]{1,0:T(2,128)S(1)}, f32[2,1024]{1,0:T(2,128)S(1)}, u32[]{:S(2)}, u32[]{:S(2)}) collective-permute-start(f32[2,1024]{1,0:T(2,128)S(1)} %add.31.refs_0_), channel_id=1, source_target_pairs={{0,192},{64,0},{128,64},{192,128},{32,96},{96,160},{160,224},{224,... | collective-permute-start | bytes 24584 | tf_op jit(solution)/shard_map/ppermute | solution.py:437
  45.4 3.5 %collective-permute-start.10 = (f32[2,1024]{1,0:T(2,128)S(1)}, f32[2,1024]{1,0:T(2,128)S(1)}, u32[]{:S(2)}, u32[]{:S(2)}) collective-permute-start(f32[2,1024]{1,0:T(2,128)S(1)} %get-tuple-element.36), channel_id=1, source_target_pairs={{0,1},{2,3},{1,0},{3,2},{4,5},{6,7},{5,4},{7,6},{8,9},{10,11},{9,8... | collective-permute-start | bytes 24584 | tf_op jit(solution)/shard_map/ppermute | solution.py:440
  49.0 0.0 collective-permute-done.18.refs_3_
  49.0 0.8 %collective-permute-start.16 = (f32[2,1024]{1,0:T(2,128)S(1)}, f32[2,1024]{1,0:T(2,128)S(1)}, u32[]{:S(2)}, u32[]{:S(2)}) collective-permute-start(f32[2,1024]{1,0:T(2,128)S(1)} %add.31.refs_0_), channel_id=1, source_target_pairs={{0,160},{32,128},{64,224},{96,192},{160,0},{128,32},{224,64},{192,... | collective-permute-start | bytes 24584 | tf_op jit(solution)/shard_map/ppermute | solution.py:437
  49.7 0.0 collective-permute-done.17.refs_2_
  49.7 3.7 %collective-permute-start.11 = (f32[2,1024]{1,0:T(2,128)S(1)}, f32[2,1024]{1,0:T(2,128)S(1)}, u32[]{:S(2)}, u32[]{:S(2)}) collective-permute-start(f32[2,1024]{1,0:T(2,128)S(1)} %get-tuple-element.37), channel_id=1, source_target_pairs={{1,2},{2,1},{0,0},{3,3},{5,6},{6,5},{4,4},{7,7},{9,10},{10,9},{8,8... | collective-permute-start | bytes 24584 | tf_op jit(solution)/shard_map/ppermute | solution.py:441
  53.4 2.2 %collective-permute-done.16.refs_1_ = f32[2,1024]{1,0:T(2,128)S(1)} collective-permute-done((f32[2,1024]{1,0:T(2,128)S(1)}, f32[2,1024]{1,0:T(2,128)S(1)}, u32[]{:S(2)}, u32[]{:S(2)}) %collective-permute-start.16) | collective-permute-done | bytes 8224 | tf_op jit(solution)/shard_map/ppermute | solution.py:437
  55.6 0.8 %scaled.1 = f32[16,128]{1,0:T(8,128)} custom-call(f32[2,1024]{1,0:T(2,128)S(1)} %add.31.refs_0_, f32[2,1024]{1,0:T(2,128)S(1)} %collective-permute-done.16.refs_1_, f32[2,1024]{1,0:T(2,128)S(1)} %collective-permute-done.17.refs_2_, f32[2,1024]{1,0:T(2,128)S(1)} %collective-permute-done.18.refs_3_), custom_call_target="tpu_custom_call" | custom-call | tf_op jit(solution)/shard_map/scaled/pallas_call | solution.py:379
  56.4 0.0 collective-permute-done.10.ue_ref
  56.4 0.0 collective-permute-done.11.uo_ref
  56.4 0.0 collective-permute-done.4.us_ref
  56.4 0.0 collective-permute-done.9.uc_ref
  56.4 0.9 %halo.1 = f32[2,64,1024]{2,1,0:T(8,128)} custom-call(f32[2,64,1024]{2,1,0:T(8,128)S(1)} %get-tuple-element.27.base_ref, f32[2,64,1024]{2,1,0:T(8,128)S(1)} %get-tuple-element.28.wz_ref, f32[4,1024]{1,0:T(4,128)S(1)} %get-tuple-element.29.wy_ref, f32[64,1024]{1,0:T(8,128)S(1)} %collective-permute-done.4.us_ref, f32[64,1024]{1,0:T(8,128)S(1)} %collective-permute-done.9.uc_ref, ...), custom_call_target="tpu_custom_call" | custom-call | flops 1048576 | bytes 2097152 | tf_op jit(solution)/shard_map/halo/pallas_call | solution.py:356
  (5 shorter events, 0.0 us)
Async XLA Ops:
  0.6 11.0 %copy-start.5 = (f32[32]{0:T(128)S(1)}, f32[32]{0:T(128)}, u32[]{:S(2)}) copy-start(f32[32]{0:T(128)} %param.9) | copy-start | bytes 388
  0.6 11.0 %slice-start = ((s8[8388608]{0:T(1024)(128)(4,1)}), s8[4194304]{0:T(1024)(128)(4,1)S(1)}, s32[]{:S(2)}) async-start(s8[8388608]{0:T(1024)(128)(4,1)} %bitcast.29), calls=%async_computation | async-start | bytes 8388608
  0.7 11.0 %copy-start = (f32[2,64,1024]{2,1,0:T(8,128)S(1)}, f32[2,64,1024]{2,1,0:T(8,128)}, u32[]{:S(2)}) copy-start(f32[2,64,1024]{2,1,0:T(8,128)} %param.7) | copy-start | bytes 1572868
  0.7 11.0 %slice-start.1 = ((s8[8388608]{0:T(1024)(128)(4,1)}), s8[4194304]{0:T(1024)(128)(4,1)S(1)}, s32[]{:S(2)}) async-start(s8[8388608]{0:T(1024)(128)(4,1)} %bitcast.29), calls=%async_computation.1 | async-start | bytes 8388608
  2.1 11.8 %copy-start.1 = (f32[2,64,1024]{2,1,0:T(8,128)S(1)}, f32[2,64,1024]{2,1,0:T(8,128)}, u32[]{:S(2)}) copy-start(f32[2,64,1024]{2,1,0:T(8,128)} %k_ref.1) | copy-start | bytes 1572868
  2.1 11.8 %copy-start.2 = (f32[2,64,1024]{2,1,0:T(8,128)S(1)}, f32[2,64,1024]{2,1,0:T(8,128)}, u32[]{:S(2)}) copy-start(f32[2,64,1024]{2,1,0:T(8,128)} %rhs_ref.1) | copy-start | bytes 1572868
  2.1 11.8 %copy-start.3 = (s32[2,64,8]{1,2,0:T(8,128)S(1)}, s32[2,64,8]{1,2,0:T(8,128)}, u32[]{:S(2)}) copy-start(s32[2,64,8]{1,2,0:T(8,128)} %param.12) | copy-start | bytes 12292
  2.1 11.8 %copy-start.4 = (s32[2,64,8]{1,2,0:T(8,128)S(1)}, s32[2,64,8]{1,2,0:T(8,128)}, u32[]{:S(2)}) copy-start(s32[2,64,8]{1,2,0:T(8,128)} %param.13) | copy-start | bytes 12292
  2.1 11.7 %collective-permute-start = (f32[72,1024]{1,0:T(8,128)S(1)}, f32[72,1024]{1,0:T(8,128)S(1)}, u32[]{:S(2)}, u32[]{:S(2)}) collective-permute-start(f32[72,1024]{1,0:T(8,128)S(1)} %get-tuple-element.22), channel_id=1, source_target_pairs={{0,4},{8,12},{16,20},{24,28},{32,36},{40,44},{48,52},{56,60},{64,6... | collective-permute-start | bytes 884744 | tf_op jit(solution)/shard_map/ppermute | solution.py:422
  2.2 11.6 %collective-permute-start.1 = (f32[72,1024]{1,0:T(8,128)S(1)}, f32[72,1024]{1,0:T(8,128)S(1)}, u32[]{:S(2)}, u32[]{:S(2)}) collective-permute-start(f32[72,1024]{1,0:T(8,128)S(1)} %get-tuple-element.23), channel_id=1, source_target_pairs={{4,8},{12,16},{20,24},{28,32},{36,40},{44,48},{52,56},{60,64},{68,... | collective-permute-start | bytes 884744 | tf_op jit(solution)/shard_map/ppermute | solution.py:421
  6.8 7.0 %collective-permute-start.2 = (f32[8,1024]{1,0:T(8,128)S(1)}, f32[8,1024]{1,0:T(8,128)S(1)}, u32[]{:S(2)}, u32[]{:S(2)}) collective-permute-start(f32[8,1024]{1,0:T(8,128)S(1)} %get-tuple-element.24), channel_id=1, source_target_pairs={{0,1},{2,3},{1,0},{3,2},{4,5},{6,7},{5,4},{7,6},{8,9},{10,11},{9,8... | collective-permute-start | bytes 98312 | tf_op jit(solution)/shard_map/ppermute | solution.py:423
  7.3 6.5 %collective-permute-start.3 = (f32[8,1024]{1,0:T(8,128)S(1)}, f32[8,1024]{1,0:T(8,128)S(1)}, u32[]{:S(2)}, u32[]{:S(2)}) collective-permute-start(f32[8,1024]{1,0:T(8,128)S(1)} %get-tuple-element.25), channel_id=1, source_target_pairs={{1,2},{2,1},{0,0},{3,3},{5,6},{6,5},{4,4},{7,7},{9,10},{10,9},{8,8... | collective-permute-start | bytes 98312 | tf_op jit(solution)/shard_map/ppermute | solution.py:424
  16.5 1.3 %collective-permute-start.5 = (f32[2,1024]{1,0:T(2,128)S(1)}, f32[2,1024]{1,0:T(2,128)S(1)}, u32[]{:S(2)}, u32[]{:S(2)}) collective-permute-start(f32[2,1024]{1,0:T(2,128)S(1)} %get-tuple-element.34), channel_id=1, source_target_pairs={{0,4},{8,12},{16,20},{24,28},{32,36},{40,44},{48,52},{56,60},{64,6... | collective-permute-start | bytes 24584 | tf_op jit(solution)/shard_map/ppermute | solution.py:430
  17.8 3.7 %collective-permute-start.8 = (f32[2,1024]{1,0:T(2,128)S(1)}, f32[2,1024]{1,0:T(2,128)S(1)}, u32[]{:S(2)}, u32[]{:S(2)}) collective-permute-start(f32[2,1024]{1,0:T(2,128)S(1)} %add.24), channel_id=1, source_target_pairs={{0,1},{1,0},{2,3},{3,2},{4,5},{5,4},{6,7},{7,6},{8,9},{9,8},{10,11... | collective-permute-start | bytes 24584 | tf_op jit(solution)/shard_map/ppermute | solution.py:437
  17.8 5.2 %collective-permute-start.7 = (f32[2,1024]{1,0:T(2,128)S(1)}, f32[2,1024]{1,0:T(2,128)S(1)}, u32[]{:S(2)}, u32[]{:S(2)}) collective-permute-start(f32[2,1024]{1,0:T(2,128)S(1)} %add.24), channel_id=1, source_target_pairs={{0,2},{1,3},{2,0},{3,1},{4,6},{5,7},{6,4},{7,5},{8,10},{9,11},{10,... | collective-permute-start | bytes 24584 | tf_op jit(solution)/shard_map/ppermute | solution.py:437
  20.9 3.7 %collective-permute-start.6 = (f32[2,1024]{1,0:T(2,128)S(1)}, f32[2,1024]{1,0:T(2,128)S(1)}, u32[]{:S(2)}, u32[]{:S(2)}) collective-permute-start(f32[2,1024]{1,0:T(2,128)S(1)} %add.24), channel_id=1, source_target_pairs={{0,3},{1,2},{2,1},{3,0},{4,7},{5,6},{6,5},{7,4},{8,11},{9,10},{10,... | collective-permute-start | bytes 24584 | tf_op jit(solution)/shard_map/ppermute | solution.py:437
  21.3 35.1 %collective-permute-start.4 = (f32[64,1024]{1,0:T(8,128)S(1)}, f32[64,1024]{1,0:T(8,128)S(1)}, u32[]{:S(2)}, u32[]{:S(2)}) collective-permute-start(f32[64,1024]{1,0:T(8,128)S(1)} %bitcast.40), channel_id=1, source_target_pairs={{0,4},{8,12},{16,20},{24,28},{32,36},{40,44},{48,52},{56,60},{64,6... | collective-permute-start | bytes 786440 | tf_op jit(solution)/shard_map/ppermute | solution.py:439
  24.6 31.8 %collective-permute-start.9 = (f32[64,1024]{1,0:T(8,128)S(1)}, f32[64,1024]{1,0:T(8,128)S(1)}, u32[]{:S(2)}, u32[]{:S(2)}) collective-permute-start(f32[64,1024]{1,0:T(8,128)S(1)} %bitcast.39), channel_id=1, source_target_pairs={{4,8},{12,16},{20,24},{28,32},{36,40},{44,48},{52,56},{60,64},{68,... | collective-permute-start | bytes 786440 | tf_op jit(solution)/shard_map/ppermute | solution.py:438
  26.5 4.8 %collective-permute-start.14 = (f32[2,1024]{1,0:T(2,128)S(1)}, f32[2,1024]{1,0:T(2,128)S(1)}, u32[]{:S(2)}, u32[]{:S(2)}) collective-permute-start(f32[2,1024]{1,0:T(2,128)S(1)} %add_add_fusion.1), channel_id=1, source_target_pairs={{0,8},{8,0},{16,24},{24,16},{1,9},{9,1},{17,25},{25,17},{2,10},{10... | collective-permute-start | bytes 24584 | tf_op jit(solution)/shard_map/ppermute | solution.py:437
  26.8 5.3 %collective-permute-start.13 = (f32[2,1024]{1,0:T(2,128)S(1)}, f32[2,1024]{1,0:T(2,128)S(1)}, u32[]{:S(2)}, u32[]{:S(2)}) collective-permute-start(f32[2,1024]{1,0:T(2,128)S(1)} %add_add_fusion.1), channel_id=1, source_target_pairs={{0,16},{8,24},{16,0},{24,8},{1,17},{9,25},{17,1},{25,9},{2,18},{10... | collective-permute-start | bytes 24584 | tf_op jit(solution)/shard_map/ppermute | solution.py:437
  29.6 5.0 %collective-permute-start.12 = (f32[2,1024]{1,0:T(2,128)S(1)}, f32[2,1024]{1,0:T(2,128)S(1)}, u32[]{:S(2)}, u32[]{:S(2)}) collective-permute-start(f32[2,1024]{1,0:T(2,128)S(1)} %add_add_fusion.1), channel_id=1, source_target_pairs={{0,24},{8,16},{16,8},{24,0},{1,25},{9,17},{17,9},{25,1},{2,26},{10... | collective-permute-start | bytes 24584 | tf_op jit(solution)/shard_map/ppermute | solution.py:437
  34.7 3.7 %collective-permute-start.15 = (f32[2,1024]{1,0:T(2,128)S(1)}, f32[2,1024]{1,0:T(2,128)S(1)}, u32[]{:S(2)}, u32[]{:S(2)}) collective-permute-start(f32[2,1024]{1,0:T(2,128)S(1)} %add_add_fusion), channel_id=1, source_target_pairs={{0,32},{64,96},{128,160},{192,224},{32,0},{96,64},{160,128},{224,1... | collective-permute-start | bytes 24584 | tf_op jit(solution)/shard_map/ppermute | solution.py:437
  38.4 10.5 %collective-permute-start.18 = (f32[2,1024]{1,0:T(2,128)S(1)}, f32[2,1024]{1,0:T(2,128)S(1)}, u32[]{:S(2)}, u32[]{:S(2)}) collective-permute-start(f32[2,1024]{1,0:T(2,128)S(1)} %add.31.refs_0_), channel_id=1, source_target_pairs={{32,64},{96,128},{160,192},{224,0},{64,32},{128,96},{192,160},{0,2... | collective-permute-start | bytes 24584 | tf_op jit(solution)/shard_map/ppermute | solution.py:437
  41.3 8.5 %collective-permute-start.17 = (f32[2,1024]{1,0:T(2,128)S(1)}, f32[2,1024]{1,0:T(2,128)S(1)}, u32[]{:S(2)}, u32[]{:S(2)}) collective-permute-start(f32[2,1024]{1,0:T(2,128)S(1)} %add.31.refs_0_), channel_id=1, source_target_pairs={{0,192},{64,0},{128,64},{192,128},{32,96},{96,160},{160,224},{224,... | collective-permute-start | bytes 24584 | tf_op jit(solution)/shard_map/ppermute | solution.py:437
  45.4 10.9 %collective-permute-start.10 = (f32[2,1024]{1,0:T(2,128)S(1)}, f32[2,1024]{1,0:T(2,128)S(1)}, u32[]{:S(2)}, u32[]{:S(2)}) collective-permute-start(f32[2,1024]{1,0:T(2,128)S(1)} %get-tuple-element.36), channel_id=1, source_target_pairs={{0,1},{2,3},{1,0},{3,2},{4,5},{6,7},{5,4},{7,6},{8,9},{10,11},{9,8... | collective-permute-start | bytes 24584 | tf_op jit(solution)/shard_map/ppermute | solution.py:440
  49.0 6.7 %collective-permute-start.16 = (f32[2,1024]{1,0:T(2,128)S(1)}, f32[2,1024]{1,0:T(2,128)S(1)}, u32[]{:S(2)}, u32[]{:S(2)}) collective-permute-start(f32[2,1024]{1,0:T(2,128)S(1)} %add.31.refs_0_), channel_id=1, source_target_pairs={{0,160},{32,128},{64,224},{96,192},{160,0},{128,32},{224,64},{192,... | collective-permute-start | bytes 24584 | tf_op jit(solution)/shard_map/ppermute | solution.py:437
  49.7 6.6 %collective-permute-start.11 = (f32[2,1024]{1,0:T(2,128)S(1)}, f32[2,1024]{1,0:T(2,128)S(1)}, u32[]{:S(2)}, u32[]{:S(2)}) collective-permute-start(f32[2,1024]{1,0:T(2,128)S(1)} %get-tuple-element.37), channel_id=1, source_target_pairs={{1,2},{2,1},{0,0},{3,3},{5,6},{6,5},{4,4},{7,7},{9,10},{10,9},{8,8... | collective-permute-start | bytes 24584 | tf_op jit(solution)/shard_map/ppermute | solution.py:441
